TPU v7x, 256 devices: a whole 4x4x8 slice. The times are simulated.
256 devices in a mesh: row: 16 (over z_hi, y), col: 16 (over z_lo, x, core).
Axes of the slice: x: 4, y: 4, z: 8 (z_hi: 4, z_lo: 2; z = z_hi * 2 + z_lo), core: 2. Of those that a mesh axis runs over, the one named last changes fastest.
Arguments:
- tokens: bfloat16 [8192, 4096], P('row', 'col'), may hold values from -6 to 6
- norm_gain: bfloat16 [4096], P('col'), may hold values from 0.099609375 to 1.8984375
- gate_weight: bfloat16 [4096, 10240], P('row', 'col'), may hold values from -0.09375 to 0.09375
- linear_weight: bfloat16 [4096, 10240], P('row', 'col'), may hold values from -0.09375 to 0.09375
- output_weight: bfloat16 [10240, 4096], P('col', 'row'), may hold values from -0.078125 to 0.078125
Outputs:
- block_out: bfloat16 [8192, 4096], P('row', 'col')
All inputs are finite; a program needn't handle non-finite values.
Results may differ from a plain program's by a relative error of at most 0.0065.
Values may be sent and summed in bfloat16 or wider, within the bound.
A program may use at most 128 MiB of HBM per device.

v0:
```python
import jax
import jax.numpy as jnp
from jax import lax
from jax.sharding import PartitionSpec as P


def turned_gather(arrays, axis, dims):
    turned = [jnp.moveaxis(a, dim, 0) for a, dim in zip(arrays, dims)]
    widths = [t[0].size for t in turned]
    both = jnp.concatenate([t.reshape(-1, w) for t, w in zip(turned, widths)], axis=1)
    filled = lax.all_gather(both, axis, axis=0, tiled=True)
    parts = jnp.split(filled, [sum(widths[:k]) for k in range(1, len(widths))], axis=1)
    return tuple(
        (
            jnp.moveaxis(b.reshape(-1, *t.shape[1:]), 0, dim)
            for b, t, dim in zip(parts, turned, dims)
        )
    )


def side_by_side(arrays, axis, dim, along):
    both = jnp.concatenate(arrays, axis=along)
    filled, at, gathered = (lax.all_gather(both, axis, axis=dim, tiled=True), 0, [])
    for a in arrays:
        gathered.append(lax.slice_in_dim(filled, at, at + a.shape[along], axis=along))
        at += a.shape[along]
    return tuple(gathered)


def add_rows(left, piece):
    return jnp.dot(left, piece, preferred_element_type=jnp.float32)


def local(tokens, norm_gain, gate_weight, linear_weight, output_weight):
    whole, gain_all = turned_gather((tokens, norm_gain), "col", (1, 0))
    values = whole.astype(jnp.float32)
    meansq = jnp.mean(values * values, axis=-1, keepdims=True)
    normed = (values * lax.rsqrt(meansq + 1e-06) * gain_all.astype(jnp.float32)).astype(
        jnp.bfloat16
    )
    pieces = side_by_side((gate_weight, linear_weight), "row", 0, 1)
    gate = add_rows(normed, pieces[0])
    linear = add_rows(normed, pieces[1])
    hidden = (jax.nn.gelu(gate, approximate=True) * linear).astype(jnp.bfloat16)
    terms = jnp.dot(
        hidden,
        lax.all_gather(output_weight, "row", axis=1, tiled=True),
        preferred_element_type=jnp.float32,
    )
    return lax.psum_scatter(terms, "col", scatter_dimension=1, tiled=True).astype(jnp.bfloat16)


def solution(mesh):
    return jax.shard_map(
        local,
        mesh=mesh,
        in_specs=(P("row", "col"), P("col"), P("row", "col"), P("row", "col"), P("col", "row")),
        out_specs=P("row", "col"),
        check_vma=False,
    )
```

profile of v0, /device:TPU:6, one launch (start us, length us, event | category | flops | bytes accessed | tf_op | source)
XLA Modules:
  0.0 381.4 jit_solution(17165300564856851926)
XLA Ops:
  6.5 0.0 all-gather.4.cloned.1.call-start
  6.5 0.7 reshape.19
  7.2 1.7 pad_maximum_fusion.1
  8.9 0.0 all-gather.4.cloned.1.call-update
  8.9 0.0 all-gather.6.cloned.1.call-start
  8.9 2.0 pad_maximum_fusion
  10.9 0.0 all-gather.6.cloned.1.call-update
  10.9 0.0 all-gather.8.cloned.1.call-start
  11.0 0.7 all-gather.8.cloned.1.call-update
  11.7 0.0 reduce-scatter.2.cloned.1.call-start
  11.7 47.4 %all-gather.4.cloned.1.call-done = bf16[4096,513]{0,1:T(8,128)(2,1)} async-done(((bf16[256,513]{0,1:T(8,128)(2,1)}), bf16[4096,513]{0,1:T(8,128)(2,1)}) %all-gather.4.cloned.1.call-update) | async-done | bytes 4202512 | tf_op jit(solution)/shard_map/all_gather | solution.py:11
  59.1 0.0 slice-start
  59.1 3.1 fusion
  62.3 0.9 slice_convert_fusion
  63.1 129.3 %all-gather.6.cloned.1.call-done = bf16[4096,1280]{1,0:T(8,128)(2,1)} async-done(((bf16[256,1280]{1,0:T(8,128)(2,1)}), bf16[4096,1280]{1,0:T(8,128)(2,1)}) %all-gather.6.cloned.1.call-update) | async-done | bytes 10485776 | tf_op jit(solution)/shard_map/all_gather | solution.py:23
  192.4 0.0 slice-start.1
  192.4 0.0 copy-start
  192.4 7.1 %fusion.5 = f32[512,640]{1,0:T(8,128)S(1)} fusion(bf16[4096,1280]{1,0:T(8,128)(2,1)} %all-gather.6.cloned.1.call-done, f32[4096]{0:T(1024)S(1)} %bitcast.7, f32[512]{0:T(512)S(1)} %add_rsqrt_fusion, bf16[4096,513]{0,1:T(8,128)(2,1)} %all-gather.4.cloned.1.call-done), kind=kOutput, calls=%fused_computation.7 | convolution fusion | flops 2692743168 | bytes 10766336 | tf_op jit(solution)/shard_map/dot_general | solution.py:31
  199.4 0.0 slice-done
  199.4 0.0 slice-done.1
  199.5 0.9 copy-done
  200.3 3.7 fusion.10
  204.0 87.5 %all-gather.8.cloned.1.call-done = bf16[640,4096]{1,0:T(8,128)(2,1)} async-done(((bf16[640,256]{1,0:T(8,128)(2,1)}), bf16[640,4096]{1,0:T(8,128)(2,1)}) %all-gather.8.cloned.1.call-update) | async-done | bytes 5242896 | tf_op jit(solution)/shard_map/all_gather | solution.py:47
  291.5 8.2 %fusion.22 = f32[512,4096]{1,0:T(8,128)} fusion(bf16[512,640]{1,0:T(8,128)(2,1)S(1)} %fusion.10, bf16[640,4096]{1,0:T(8,128)(2,1)} %all-gather.8.cloned.1.call-done), kind=kOutput, calls=%fused_computation.23 | convolution fusion | flops 2684354560 | bytes 14286848 | tf_op jit(solution)/shard_map/dot_general | solution.py:45
  299.7 0.0 reduce-scatter.2.cloned.1.call-update
  299.7 73.4 %reduce-scatter.2.cloned.1.call-done = f32[512,256]{1,0:T(8,128)} async-done(((f32[512,4096]{1,0:T(8,128)}), f32[512,256]{1,0:T(8,128)}) %reduce-scatter.2.cloned.1.call-update) | async-done | bytes 524304 | tf_op jit(solution)/shard_map/reduce_scatter | solution.py:50
  373.1 1.8 convert_element_type.29
  (2 shorter events, 0.0 us)
Async XLA Ops:
  6.5 52.6 %all-gather.4.cloned.1.call-start = ((), (), s32[]{:S(2)}) async-start(), calls=%async_computation.1 | async-start | bytes 4526080 | tf_op jit(solution)/shard_map/all_gather | solution.py:11
  8.9 183.5 %all-gather.6.cloned.1.call-start = ((), (), s32[]{:S(2)}) async-start(), calls=%async_computation.2 | async-start | bytes 11141120 | tf_op jit(solution)/shard_map/all_gather | solution.py:23
  10.9 280.6 %all-gather.8.cloned.1.call-start = ((), (), s32[]{:S(2)}) async-start(), calls=%async_computation.3 | async-start | bytes 5570560 | tf_op jit(solution)/shard_map/all_gather | solution.py:47
  11.7 361.4 %reduce-scatter.2.cloned.1.call-start = ((), (), s32[]{:S(2)}) async-start(), calls=%async_computation.4 | async-start | bytes 8912896 | tf_op jit(solution)/shard_map/reduce_scatter | solution.py:50
  59.1 140.3 %slice-start = ((s8[4259840]{0:T(1024)(128)(4,1)}), s8[65536]{0:T(1024)(128)(4,1)S(1)}, s32[]{:S(2)}) async-start(s8[4259840]{0:T(1024)(128)(4,1)} %bitcast.4), calls=%async_computation.5 | async-start | bytes 131072
  192.4 7.1 %slice-start.1 = ((s8[4259840]{0:T(1024)(128)(4,1)}), s8[4194304]{0:T(1024)(128)(4,1)S(1)}, s32[]{:S(2)}) async-start(s8[4259840]{0:T(1024)(128)(4,1)} %bitcast.4), calls=%async_computation.6 | async-start | bytes 8388608
  192.4 8.0 %copy-start = (bf16[4096,1280]{1,0:T(8,128)(2,1)S(1)}, bf16[4096,1280]{1,0:T(8,128)(2,1)}, u32[]{:S(2)}) copy-start(bf16[4096,1280]{1,0:T(8,128)(2,1)} %all-gather.6.cloned.1.call-done) | copy-start | bytes 31457284
Sparse Core Ops, SparseCore 0:
  9.1 49.9 all-gather.3
  61.6 130.7 all-gather.5
  194.8 96.7 all-gather.7
  299.8 73.2 reduce-scatter.1
where the time goes:
time: 386 us; the launch traced here: 381 us
  waiting for transfers between devices  338 us (88%)
  matrix products  18.9 us (5%)
  between operations  13.2 us (3%)
  other arithmetic  9.37 us (2%)
    all_gather x1, waiting for transfers between devices, side_by_side(): lax.all_gather(both, axis, axis=dim, tiled=True)  129 us
    all_gather x1, waiting for transfers between devices, local(): lax.all_gather(output_weight, 'row', axis=1, tiled=True)  87.5 us
    reduce_scatter x1, waiting for transfers between devices, local(): lax.psum_scatter(terms, 'col', scatter_dimension=1, tiled=True)  73.4 us
    all_gather x1, waiting for transfers between devices, turned_gather(): filled = lax.all_gather(both, axis, axis=0, tiled=True)  47.4 us
    dot_general x2, matrix products, add_rows(): return jnp.dot(left, piece, preferred_element_type=jnp.float32)  10.7 us
    dot_general x1, matrix products, local(): jnp.dot(hidden, lax.all_gather(output_weight, 'row', axis=1, tiled=True),...  8.15 us
  transfers between devices with their start and end apart: 4, of which 4 were waited for; matrix products, arithmetic and copies ran while one was open for 4% of the time, Pallas kernels for 0%

commit v1 on v0

v1 whole, which is shorter than its diff:
```python
import jax
import jax.numpy as jnp
from jax import lax
from jax.experimental import pallas as pl
from jax.experimental.pallas import tpu as pltpu
from jax.sharding import PartitionSpec as P

MESH = pl.DeviceIdType.MESH
BF, F32 = jnp.bfloat16, jnp.float32
FB = 160
DB = 256
TB = 128
GR = 16
N_SEMS = 192
NT = (((1,), (1,)), ((), ()))


def wrap(v, n):
    return lax.rem(v + n, n)


def kernel(
    tok, gain, gw, lw, ow, out,
    wt, gl, w2, tst, tks, nrm, acc, hid, part, stx, srx, rtx, rrx, fin, land, send, recv,
):
    row, col = lax.axis_index("row"), lax.axis_index("col")
    zh, y = lax.div(row, 4), lax.rem(row, 4)
    zl, x, k = lax.div(col, 8), lax.rem(lax.div(col, 2), 4), lax.rem(col, 2)
    z = zh * 2 + zl

    def device(dz=0, dy=0, dx=0, dk=0):
        nz, ny, nx = wrap(z + dz, 8), wrap(y + dy, 4), wrap(x + dx, 4)
        return (lax.div(nz, 2) * 4 + ny, lax.rem(nz, 2) * 8 + nx * 2 + lax.rem(k + dk, 2))

    peers = (
        [device(dz=d) for d in (1, -1, 2, -2, 4)]
        + [device(dx=d) for d in (1, -1, 2)]
        + [device(dy=d) for d in (1, -1)]
        + [device(dk=1)]
    )
    barrier = pltpu.get_barrier_semaphore()
    for peer in peers:
        pl.semaphore_signal(barrier, inc=1, device_id=peer, device_id_type=MESH)

    wt[0] = gw[...].T
    wt[1] = lw[...].T
    for i in range(4):
        tst[i, 0:TB] = tok[i * TB : (i + 1) * TB]
        tst[i, TB : TB + GR] = jnp.broadcast_to(gain[...], (GR, DB))
    pl.semaphore_wait(barrier, len(peers))

    ids, sent = {}, []

    def copy_of(name, src, dst, to):
        i = ids.setdefault(name, len(ids))
        return pltpu.make_async_remote_copy(
            src_ref=src, dst_ref=dst, send_sem=send.at[i], recv_sem=recv.at[i],
            device_id=to, device_id_type=MESH,
        )

    def push(name, src, dst, to):
        copy = copy_of(name, src, dst, to)
        copy.start()
        sent.append(copy)

    def arrive(name, dst):
        copy_of(name, dst, dst, device(dk=1)).wait_recv()

    def token_block(dz):
        nz = wrap(z + dz, 8)
        return tks.at[lax.rem(nz, 2), k, lax.div(nz, 2)]

    def token_block_other(dz):
        nz = wrap(z + dz, 8)
        return tks.at[lax.rem(nz, 2), 1 - k, lax.div(nz, 2)]

    for e in (1, 3, 2):
        push(f"ta{4 - e}", tst.at[wrap(x + e, 4)], tks.at[zl, k, zh, x], device(dx=e))

    def rows_for(d):
        return pl.ds(pl.multiple_of(wrap(zh + d, 4) * FB, 16), FB)

    for e in (1, 3, 2):
        push(f"gz{4 - e}", wt.at[:, rows_for(e), :], gl.at[zh, y, :, x], device(dz=2 * e))
    for e in (1, 3, 2):
        push(f"wz{4 - e}", ow.at[rows_for(e), :], w2.at[zh, y, x], device(dz=2 * e))
    gl[zh, y, :, x] = wt[:, rows_for(0), :]
    w2[zh, y, x] = ow[rows_for(0), :]
    tks[zl, k, zh, x] = tst[x]

    class Unit:
        def __init__(self, kind, u, first, way):
            self.kind, self.u, self.first, self.way = kind, u, first, way
            self.tag = f"{kind}{first}{way}" if kind == "g" else f"{kind}{u}"
            self.p, self.q = (x, y) if first == "x" else (y, x)

        def block(self, df, ds):
            f, s = wrap(self.p + df, 4), wrap(self.q + ds, 4)
            yy, xx = (s, f) if self.first == "x" else (f, s)
            return gl.at[self.u, yy, :, xx] if self.kind == "g" else w2.at[self.u, yy, xx]

        def along(self, step, second=False):
            return device(dx=step) if (self.first == "x") != second else device(dy=step)

        def go(self, name, df, ds, step, second=False):
            ref = self.block(df, ds)
            push(f"{self.tag}{name}", ref, ref, self.along(step, second))

        def get(self, name, df, ds):
            arrive(f"{self.tag}{name}", self.block(df, ds))

        def spread(self, j):
            df = (0, -1, 1, 2)[j]
            self.go(f"L{j}", df, 0, 1, True)
            self.go(f"R{j}", df, 0, -1, True)

        def a0(self):
            self.go("l", 0, 0, 1)
            self.go("r", 0, 0, -1)
            self.spread(0)

        def a1(self):
            self.get("l", -1, 0)
            if self.way > 0:
                self.go("o", -1, 0, 1)
            self.spread(1)
            self.get("r", 1, 0)
            if self.way < 0:
                self.go("o", 1, 0, -1)
            self.spread(2)

        def a2(self):
            self.get("o", 2, 0)
            self.spread(3)

        def a3(self, j):
            df = (0, -1, 1, 2)[j]
            self.get(f"L{j}", df, -1)
            if j in (0, 3):
                self.go(f"O{j}", df, -1, 1, True)
            self.get(f"R{j}", df, 1)
            if j in (1, 2):
                self.go(f"O{j}", df, 1, -1, True)

        def a5(self):
            for j, df in enumerate((0, -1, 1, 2)):
                self.get(f"O{j}", df, 2)

    def each(units, stage, *args):
        for unit in units:
            getattr(unit, stage)(*args)

    def unit_of(d):
        return wrap(zh + d, 4)

    g0 = [Unit("g", unit_of(0), "x", 1), Unit("g", unit_of(1), "y", 1)]
    g1 = [Unit("g", unit_of(3), "x", -1), Unit("g", unit_of(2), "y", -1)]
    v0 = [Unit("w", 0, "x", 1), Unit("w", 2, "y", 1)]
    v1 = [Unit("w", 1, "x", -1), Unit("w", 3, "y", -1)]

    def z_arrival(name, d):
        u = unit_of(d)
        arrive(f"{name}{d}", gl.at[u, y, :, x] if name == "gz" else w2.at[u, y, x])

    def tokens_first():
        for d in (1, 3, 2):
            arrive(f"ta{d}", tks.at[zl, k, zh, wrap(x + d, 4)])
        own = token_block(0)
        push("tm1", own, own, device(dz=-1))
        push("tp1", own, own, device(dz=1))
        push("s0", own, own, device(dk=1))

    def tokens_next(m):
        block = token_block(m)
        arrive(f"tm{m}", block)
        if m < 4:
            push(f"tm{m + 1}", block, block, device(dz=-1))
        push(f"s{m}", block, block, device(dk=1))
        if m < 4:
            block = token_block(-m)
            arrive(f"tp{m}", block)
            if m < 3:
                push(f"tp{m + 1}", block, block, device(dz=1))
            push(f"s{-m}", block, block, device(dk=1))

    def tokens_last():
        for m in (0, 1, -1, 2, -2, 3, -3, 4):
            arrive(f"s{m}", token_block_other(m))

    def normalise():
        spots = [(a, b, c) for a in range(2) for b in range(2) for c in range(4)]

        @pl.loop(0, 4)
        def _(h):
            total = jnp.zeros((TB, DB), F32)
            for a, b, c in spots:
                v = tks[a, b, h, c, 0:TB, :].astype(F32)
                total = total + v * v
            mean = jnp.sum(total, axis=1, keepdims=True) * (1.0 / 4096.0)
            scale = lax.rsqrt(mean + 1e-06)
            rows = pl.ds(pl.multiple_of(h * TB, TB), TB)
            for a, b, c in spots:
                v = tks[a, b, h, c, 0:TB, :].astype(F32)
                g = tks[a, b, h, c, TB : TB + GR, :].astype(F32)[0:1, :]
                nrm[a * 8 + c * 2 + b, rows, :] = (v * scale * g).astype(BF)

    def project(unit, fresh=False):
        @pl.loop(0, 4)
        def _(t):
            left = nrm[unit.u * 4 + t]
            for a in range(2):
                term = lax.dot_general(
                    left, gl[unit.u, t, a].reshape(4 * FB, DB), NT, preferred_element_type=F32
                )
                acc[a] += term

    def activate():
        @pl.loop(0, 8)
        def _(t):
            rows = pl.ds(pl.multiple_of(t * 64, 64), 64)
            hid[rows, :] = (jax.nn.gelu(acc[0, rows, :], approximate=True) * acc[1, rows, :]).astype(BF)

    def terms(h, mine):
        core = k if mine else 1 - k

        @pl.loop(0, 4)
        def _(t):
            a, i = lax.div(t, 2), lax.rem(t, 2)
            right = w2[2 * a + h, 2 * i + core].reshape(4 * FB, DB)
            term = jnp.dot(hid[...], right, preferred_element_type=F32)
            if mine:
                part[h, a, i] = term
            else:
                stx[h, a, i] = term.astype(BF)

    def ring_value(h, dz):
        nz = wrap(z + dz, 8)
        a, rows = lax.rem(nz, 2), pl.ds(pl.multiple_of(lax.div(nz, 2) * TB, TB), TB)
        return part[h, a, :, rows, :] + srx[h, a, :, rows, :].astype(F32)

    def ring_step(h, s):
        for way in (0, 1):
            length = 4 if h == way else 3
            if s >= length:
                continue
            sign = 1 if way == 0 else -1
            value = ring_value(h, sign * (length - s))
            if s > 0:
                arrive(f"r{h}{way}{s - 1}", rrx.at[h, way, s - 1])
                value = value + rrx[h, way, s - 1].astype(F32)
            rtx[h, way, s] = value.astype(BF)
            push(f"r{h}{way}{s}", rtx.at[h, way, s], rrx.at[h, way, s], device(dz=sign))

    def ring_end(h):
        value = ring_value(h, 0)
        for way in (0, 1):
            last = 3 if h == way else 2
            arrive(f"r{h}{way}{last}", rrx.at[h, way, last])
            value = value + rrx[h, way, last].astype(F32)
        fin[2 * h : 2 * h + 2] = value.astype(BF)

    def sum_first(h):
        terms(h, False)
        push(f"c{h}", stx.at[h], srx.at[h], device(dk=1))
        terms(h, True)
        arrive(f"c{h}", srx.at[h])

    each(g0[:1], "a0")
    acc[...] = jnp.zeros_like(acc)
    tokens_first()
    z_arrival("gz", 1)
    each(g0[1:], "a0")
    each(g0, "a1")
    tokens_next(1)
    each(g0, "a2")
    each(g0, "a3", 0)
    each(g0, "a3", 1)
    tokens_next(2)
    z_arrival("gz", 3)
    z_arrival("gz", 2)
    each(g1, "a0")
    each(g0, "a3", 2)
    each(g0, "a3", 3)
    tokens_next(3)
    each(g1, "a1")
    each(g1, "a2")
    tokens_next(4)
    each(g0, "a5")
    for d in (1, 3, 2):
        z_arrival("wz", d)
    each(g1, "a3", 0)
    each(v0, "a0")
    tokens_last()
    normalise()
    each(g1, "a3", 1)
    each(g1, "a3", 2)
    project(g0[0])
    each(g1, "a3", 3)
    project(g0[1])
    each(v0, "a1")
    each(v0, "a2")
    each(v1, "a0")
    each(g1, "a5")
    project(g1[0])
    each(v0, "a3", 0)
    each(v0, "a3", 1)
    project(g1[1])
    each(v0, "a3", 2)
    each(v0, "a3", 3)
    each(v1, "a1")
    each(v1, "a2")
    activate()
    each(v0, "a5")
    sum_first(0)
    ring_step(0, 0)
    each(v1, "a3", 0)
    each(v1, "a3", 1)
    ring_step(0, 1)
    each(v1, "a3", 2)
    each(v1, "a3", 3)
    ring_step(0, 2)
    each(v1, "a5")
    sum_first(1)
    ring_step(1, 0)
    ring_step(0, 3)
    ring_step(1, 1)
    ring_end(0)
    ring_step(1, 2)
    ring_step(1, 3)
    ring_end(1)
    for e in (1, 3, 2):
        push(f"f{4 - e}", fin.at[wrap(x + e, 4)], land.at[x], device(dx=e))
    land[x] = fin[x]
    for d in (1, 3, 2):
        arrive(f"f{d}", land.at[wrap(x + d, 4)])
    out[...] = land[...].reshape(4 * TB, DB)
    for copy in sent:
        copy.wait_send()
    assert len(ids) <= N_SEMS, len(ids)


def local(tokens, norm_gain, gate_weight, linear_weight, output_weight):
    vmem = pl.BlockSpec(memory_space=pltpu.VMEM)
    return pl.pallas_call(
        kernel,
        out_shape=jax.ShapeDtypeStruct((4 * TB, DB), BF),
        in_specs=[vmem] * 5,
        out_specs=vmem,
        scratch_shapes=[
            pltpu.VMEM((2, 4 * FB, DB), BF),
            pltpu.VMEM((4, 4, 2, 4, FB, DB), BF),
            pltpu.VMEM((4, 4, 4, FB, DB), BF),
            pltpu.VMEM((4, TB + GR, DB), BF),
            pltpu.VMEM((2, 2, 4, 4, TB + GR, DB), BF),
            pltpu.VMEM((16, 4 * TB, DB), BF),
            pltpu.VMEM((2, 4 * TB, 4 * FB), F32),
            pltpu.VMEM((4 * TB, 4 * FB), BF),
            pltpu.VMEM((2, 2, 2, 4 * TB, DB), F32),
            pltpu.VMEM((2, 2, 2, 4 * TB, DB), BF),
            pltpu.VMEM((2, 2, 2, 4 * TB, DB), BF),
            pltpu.VMEM((2, 2, 4, 2, TB, DB), BF),
            pltpu.VMEM((2, 2, 4, 2, TB, DB), BF),
            pltpu.VMEM((4, TB, DB), BF),
            pltpu.VMEM((4, TB, DB), BF),
            pltpu.SemaphoreType.DMA((N_SEMS,)),
            pltpu.SemaphoreType.DMA((N_SEMS,)),
        ],
        compiler_params=pltpu.CompilerParams(
            collective_id=0, has_side_effects=True, vmem_limit_bytes=60 * 1024 * 1024
        ),
    )(tokens, norm_gain.reshape(1, DB), gate_weight, linear_weight, output_weight)


def solution(mesh):
    return jax.shard_map(
        local,
        mesh=mesh,
        in_specs=(P("row", "col"), P("col"), P("row", "col"), P("row", "col"), P("col", "row")),
        out_specs=P("row", "col"),
        check_vma=False,
    )
```

time: 386 us -> 152 us (0.39)
  waiting for transfers between devices: 338 us -> 0 us
  Pallas kernels: 0 us -> 148 us
  matrix products: 18.9 us -> 0 us
  between operations: 13.2 us -> 0.01 us
  other arithmetic: 9.37 us -> 0 us
    all_gather x3 -> x0, waiting for transfers between devices: 264 us -> none  [the longest x1 129 us: side_by_side(): lax.all_gather(both, axis, axis=dim, tiled=True)]
    pallas_call x0 -> x1, Pallas kernels: none -> 148 us  [local(): pl.pallas_call(kernel, out_shape=jax.ShapeDtypeStruct((4 * TB, DB), BF),...]
    reduce_scatter x1 -> x0, waiting for transfers between devices: 73.4 us -> none  [local(): lax.psum_scatter(terms, 'col', scatter_dimension=1, tiled=True)]
    dot_general x3 -> x0, matrix products: 18.9 us -> none  [the longest x2 10.7 us: add_rows(): return jnp.dot(left, piece, preferred_element_type=jnp.float32)]
  transfers between devices with their start and end apart: 4 -> 0, of which waited for: 4 -> 0; matrix products, arithmetic and copies ran while one was open for 4% -> 0% of each run, Pallas kernels for 0% -> 0%
where the time goes in v1:
time: 152 us; the launch traced here: 151 us
  Pallas kernels  148 us (97%)
  local copies, waits for them, and re-layouts  2.89 us (2%)
    pallas_call x1, Pallas kernels, local(): pl.pallas_call(kernel, out_shape=jax.ShapeDtypeStruct((4 * TB, DB), BF),...  148 us

profile of v1, /device:TPU:6, one launch (start us, length us, event | category | flops | bytes accessed | tf_op | source)
XLA Modules:
  0.0 150.8 jit_solution(11730291506186776748)
XLA Ops:
  0.0 1.2 reshape.3.gain
  1.2 147.9 %shard_map.55 = bf16[512,256]{1,0:T(8,128)(2,1)} custom-call(bf16[512,256]{1,0:T(8,128)(2,1)} %tok.1, bf16[1,256]{1,0:T(2,128)(2,1)} %reshape.3.gain, bf16[256,640]{1,0:T(8,128)(2,1)} %gw.1, bf16[256,640]{1,0:T(8,128)(2,1)} %lw.1, bf16[640,256]{1,0:T(8,128)(2,1)} %ow.1), custom_call_target="tpu_custom_call" | custom-call | tf_op jit(solution)/shard_map/pallas_call | solution.py:344
  149.2 1.7 %copy.7 = bf16[512,256]{1,0:T(8,128)(2,1)} copy(bf16[512,256]{1,0:T(8,128)(2,1)} %shard_map.55) | data formatting | bytes 524288

commit v2 on v1

--- a/solution.py
+++ b/solution.py
@@ -9,9 +9,10 @@
 BF, F32 = jnp.bfloat16, jnp.float32
 FB = 160
 DB = 256
+HB = DB // 2
 TB = 128
 GR = 16
-N_SEMS = 192
+N_SEMS = 320
 NT = (((1,), (1,)), ((), ()))
 
 
@@ -83,21 +84,26 @@
     for e in (1, 3, 2):
         push(f"gz{4 - e}", wt.at[:, rows_for(e), :], gl.at[zh, y, :, x], device(dz=2 * e))
     for e in (1, 3, 2):
-        push(f"wz{4 - e}", ow.at[rows_for(e), :], w2.at[zh, y, x], device(dz=2 * e))
+        for c in range(2):
+            half = pl.ds(c * HB, HB)
+            push(f"wz{c}{4 - e}", ow.at[rows_for(e), half], w2.at[c, zh, y, x], device(dz=2 * e))
     gl[zh, y, :, x] = wt[:, rows_for(0), :]
-    w2[zh, y, x] = ow[rows_for(0), :]
+    for c in range(2):
+        w2[c, zh, y, x] = ow[rows_for(0), c * HB : (c + 1) * HB]
     tks[zl, k, zh, x] = tst[x]
 
     class Unit:
-        def __init__(self, kind, u, first, way):
+        def __init__(self, kind, u, tag, first, way):
             self.kind, self.u, self.first, self.way = kind, u, first, way
-            self.tag = f"{kind}{first}{way}" if kind == "g" else f"{kind}{u}"
+            self.tag = f"k{kind}{tag}"
             self.p, self.q = (x, y) if first == "x" else (y, x)
 
         def block(self, df, ds):
             f, s = wrap(self.p + df, 4), wrap(self.q + ds, 4)
             yy, xx = (s, f) if self.first == "x" else (f, s)
-            return gl.at[self.u, yy, :, xx] if self.kind == "g" else w2.at[self.u, yy, xx]
+            if self.kind < 2:
+                return gl.at[self.u, yy, self.kind, xx]
+            return w2.at[self.kind - 2, self.u, yy, xx]
 
         def along(self, step, second=False):
             return device(dx=step) if (self.first == "x") != second else device(dy=step)
@@ -153,14 +159,25 @@
     def unit_of(d):
         return wrap(zh + d, 4)
 
-    g0 = [Unit("g", unit_of(0), "x", 1), Unit("g", unit_of(1), "y", 1)]
-    g1 = [Unit("g", unit_of(3), "x", -1), Unit("g", unit_of(2), "y", -1)]
-    v0 = [Unit("w", 0, "x", 1), Unit("w", 2, "y", 1)]
-    v1 = [Unit("w", 1, "x", -1), Unit("w", 3, "y", -1)]
-
-    def z_arrival(name, d):
-        u = unit_of(d)
-        arrive(f"{name}{d}", gl.at[u, y, :, x] if name == "gz" else w2.at[u, y, x])
+    def pair(n, d):
+        way = 1 if n % 2 == 0 else -1
+        return [Unit(0, unit_of(d), d, "x", way), Unit(1, unit_of(d), d, "y", way)]
+
+    g = [pair(n, d) for n, d in enumerate((0, 1, 3, 2))]
+    v = [
+        [
+            [Unit(2 + c, h, h, "x", 1 - 2 * h), Unit(2 + c, 2 + h, 2 + h, "y", 1 - 2 * h)]
+            for h in range(2)
+        ]
+        for c in range(2)
+    ]
+
+    def weights_in(d):
+        arrive(f"gz{d}", gl.at[unit_of(d), y, :, x])
+
+    def outputs_in(c):
+        for d in (1, 3, 2):
+            arrive(f"wz{c}{d}", w2.at[c, unit_of(d), y, x])
 
     def tokens_first():
         for d in (1, 3, 2):
@@ -204,15 +221,15 @@
                 g = tks[a, b, h, c, TB : TB + GR, :].astype(F32)[0:1, :]
                 nrm[a * 8 + c * 2 + b, rows, :] = (v * scale * g).astype(BF)
 
-    def project(unit, fresh=False):
+    def project(n):
+        u = g[n][0].u
+
         @pl.loop(0, 4)
         def _(t):
-            left = nrm[unit.u * 4 + t]
+            left = nrm[u * 4 + t]
             for a in range(2):
-                term = lax.dot_general(
-                    left, gl[unit.u, t, a].reshape(4 * FB, DB), NT, preferred_element_type=F32
-                )
-                acc[a] += term
+                right = gl[u, t, a].reshape(4 * FB, DB)
+                acc[a] += lax.dot_general(left, right, NT, preferred_element_type=F32)
 
     def activate():
         @pl.loop(0, 8)
@@ -220,120 +237,146 @@
             rows = pl.ds(pl.multiple_of(t * 64, 64), 64)
             hid[rows, :] = (jax.nn.gelu(acc[0, rows, :], approximate=True) * acc[1, rows, :]).astype(BF)
 
-    def terms(h, mine):
+    def terms(c, mine):
         core = k if mine else 1 - k
 
         @pl.loop(0, 4)
         def _(t):
-            a, i = lax.div(t, 2), lax.rem(t, 2)
-            right = w2[2 * a + h, 2 * i + core].reshape(4 * FB, DB)
+            h, a = lax.div(t, 2), lax.rem(t, 2)
+            blocks = [w2[c, 2 * a + h, 2 * i + core].reshape(4 * FB, HB) for i in range(2)]
+            right = jnp.concatenate(blocks, axis=1)
             term = jnp.dot(hid[...], right, preferred_element_type=F32)
             if mine:
-                part[h, a, i] = term
+                part[c, h, a] = term
             else:
-                stx[h, a, i] = term.astype(BF)
-
-    def ring_value(h, dz):
+                stx[c, h, a] = term.astype(BF)
+
+    def ring_value(c, h, dz):
         nz = wrap(z + dz, 8)
         a, rows = lax.rem(nz, 2), pl.ds(pl.multiple_of(lax.div(nz, 2) * TB, TB), TB)
-        return part[h, a, :, rows, :] + srx[h, a, :, rows, :].astype(F32)
-
-    def ring_step(h, s):
-        for way in (0, 1):
-            length = 4 if h == way else 3
-            if s >= length:
-                continue
-            sign = 1 if way == 0 else -1
-            value = ring_value(h, sign * (length - s))
-            if s > 0:
-                arrive(f"r{h}{way}{s - 1}", rrx.at[h, way, s - 1])
-                value = value + rrx[h, way, s - 1].astype(F32)
-            rtx[h, way, s] = value.astype(BF)
-            push(f"r{h}{way}{s}", rtx.at[h, way, s], rrx.at[h, way, s], device(dz=sign))
-
-    def ring_end(h):
-        value = ring_value(h, 0)
-        for way in (0, 1):
-            last = 3 if h == way else 2
-            arrive(f"r{h}{way}{last}", rrx.at[h, way, last])
-            value = value + rrx[h, way, last].astype(F32)
-        fin[2 * h : 2 * h + 2] = value.astype(BF)
-
-    def sum_first(h):
-        terms(h, False)
-        push(f"c{h}", stx.at[h], srx.at[h], device(dk=1))
-        terms(h, True)
-        arrive(f"c{h}", srx.at[h])
-
-    each(g0[:1], "a0")
+        return part[c, h, a, rows, :] + srx[c, h, a, rows, :].astype(F32)
+
+    def ring_step(c, s):
+        for h in (0, 1):
+            for way in (0, 1):
+                length = 4 if h == way else 3
+                if s >= length:
+                    continue
+                sign = 1 if way == 0 else -1
+                value = ring_value(c, h, sign * (length - s))
+                if s > 0:
+                    arrive(f"r{c}{h}{way}{s - 1}", rrx.at[c, h, way, s - 1])
+                    value = value + rrx[c, h, way, s - 1].astype(F32)
+                rtx[c, h, way, s] = value.astype(BF)
+                push(f"r{c}{h}{way}{s}", rtx.at[c, h, way, s], rrx.at[c, h, way, s], device(dz=sign))
+
+    def ring_end(c):
+        for h in (0, 1):
+            value = ring_value(c, h, 0)
+            for way in (0, 1):
+                last = 3 if h == way else 2
+                arrive(f"r{c}{h}{way}{last}", rrx.at[c, h, way, last])
+                value = value + rrx[c, h, way, last].astype(F32)
+            for i in range(2):
+                fin[c, 2 * h + i] = value[:, i * HB : (i + 1) * HB].astype(BF)
+        for e in (1, 3, 2):
+            push(f"f{c}{4 - e}", fin.at[c, wrap(x + e, 4)], land.at[c, x], device(dx=e))
+        land[c, x] = fin[c, x]
+
+    def finish(c):
+        for d in (1, 3, 2):
+            arrive(f"f{c}{d}", land.at[c, wrap(x + d, 4)])
+        out[:, c * HB : (c + 1) * HB] = land[c].reshape(4 * TB, HB)
+
+    def sum_first(c):
+        terms(c, False)
+        push(f"c{c}", stx.at[c], srx.at[c], device(dk=1))
+        terms(c, True)
+        arrive(f"c{c}", srx.at[c])
+
+    def reach(units, *js):
+        for j in js:
+            each(units, "a3", j)
+
+    each(g[0], "a0")
     acc[...] = jnp.zeros_like(acc)
     tokens_first()
-    z_arrival("gz", 1)
-    each(g0[1:], "a0")
-    each(g0, "a1")
+    each(g[0], "a1")
+    each(g[0], "a2")
+    weights_in(1)
+    each(g[1], "a0")
+    reach(g[0], 0, 1)
     tokens_next(1)
-    each(g0, "a2")
-    each(g0, "a3", 0)
-    each(g0, "a3", 1)
+    each(g[1], "a1")
+    reach(g[0], 2, 3)
+    each(g[1], "a2")
+    weights_in(3)
+    each(g[2], "a0")
     tokens_next(2)
-    z_arrival("gz", 3)
-    z_arrival("gz", 2)
-    each(g1, "a0")
-    each(g0, "a3", 2)
-    each(g0, "a3", 3)
+    each(g[0], "a5")
+    reach(g[1], 0, 1)
+    each(g[2], "a1")
+    reach(g[1], 2, 3)
+    each(g[2], "a2")
     tokens_next(3)
-    each(g1, "a1")
-    each(g1, "a2")
+    weights_in(2)
+    each(g[3], "a0")
+    each(g[1], "a5")
+    reach(g[2], 0, 1)
     tokens_next(4)
-    each(g0, "a5")
-    for d in (1, 3, 2):
-        z_arrival("wz", d)
-    each(g1, "a3", 0)
-    each(v0, "a0")
+    each(g[3], "a1")
+    reach(g[2], 2, 3)
+    each(g[3], "a2")
+    outputs_in(0)
+    each(v[0][0], "a0")
+    each(g[2], "a5")
     tokens_last()
     normalise()
-    each(g1, "a3", 1)
-    each(g1, "a3", 2)
-    project(g0[0])
-    each(g1, "a3", 3)
-    project(g0[1])
-    each(v0, "a1")
-    each(v0, "a2")
-    each(v1, "a0")
-    each(g1, "a5")
-    project(g1[0])
-    each(v0, "a3", 0)
-    each(v0, "a3", 1)
-    project(g1[1])
-    each(v0, "a3", 2)
-    each(v0, "a3", 3)
-    each(v1, "a1")
-    each(v1, "a2")
+    reach(g[3], 0, 1)
+    each(v[0][0], "a1")
+    project(0)
+    reach(g[3], 2, 3)
+    each(v[0][0], "a2")
+    each(v[0][1], "a0")
+    project(1)
+    each(g[3], "a5")
+    reach(v[0][0], 0, 1)
+    each(v[0][1], "a1")
+    project(2)
+    reach(v[0][0], 2, 3)
+    each(v[0][1], "a2")
+    outputs_in(1)
+    each(v[1][0], "a0")
+    project(3)
+    each(v[0][0], "a5")
+    reach(v[0][1], 0, 1)
+    each(v[1][0], "a1")
     activate()
-    each(v0, "a5")
+    reach(v[0][1], 2, 3)
+    each(v[1][0], "a2")
+    each(v[1][1], "a0")
+    each(v[0][1], "a5")
     sum_first(0)
     ring_step(0, 0)
-    each(v1, "a3", 0)
-    each(v1, "a3", 1)
+    reach(v[1][0], 0, 1, 2, 3)
+    each(v[1][1], "a1")
+    each(v[1][1], "a2")
     ring_step(0, 1)
-    each(v1, "a3", 2)
-    each(v1, "a3", 3)
+    each(v[1][0], "a5")
+    reach(v[1][1], 0, 1)
     ring_step(0, 2)
-    each(v1, "a5")
+    reach(v[1][1], 2, 3)
+    ring_step(0, 3)
+    each(v[1][1], "a5")
     sum_first(1)
     ring_step(1, 0)
-    ring_step(0, 3)
+    ring_end(0)
     ring_step(1, 1)
-    ring_end(0)
     ring_step(1, 2)
     ring_step(1, 3)
     ring_end(1)
-    for e in (1, 3, 2):
-        push(f"f{4 - e}", fin.at[wrap(x + e, 4)], land.at[x], device(dx=e))
-    land[x] = fin[x]
-    for d in (1, 3, 2):
-        arrive(f"f{d}", land.at[wrap(x + d, 4)])
-    out[...] = land[...].reshape(4 * TB, DB)
+    finish(0)
+    finish(1)
     for copy in sent:
         copy.wait_send()
     assert len(ids) <= N_SEMS, len(ids)
@@ -349,7 +392,7 @@
         scratch_shapes=[
             pltpu.VMEM((2, 4 * FB, DB), BF),
             pltpu.VMEM((4, 4, 2, 4, FB, DB), BF),
-            pltpu.VMEM((4, 4, 4, FB, DB), BF),
+            pltpu.VMEM((2, 4, 4, 4, FB, HB), BF),
             pltpu.VMEM((4, TB + GR, DB), BF),
             pltpu.VMEM((2, 2, 4, 4, TB + GR, DB), BF),
             pltpu.VMEM((16, 4 * TB, DB), BF),
@@ -358,10 +401,10 @@
             pltpu.VMEM((2, 2, 2, 4 * TB, DB), F32),
             pltpu.VMEM((2, 2, 2, 4 * TB, DB), BF),
             pltpu.VMEM((2, 2, 2, 4 * TB, DB), BF),
-            pltpu.VMEM((2, 2, 4, 2, TB, DB), BF),
-            pltpu.VMEM((2, 2, 4, 2, TB, DB), BF),
-            pltpu.VMEM((4, TB, DB), BF),
-            pltpu.VMEM((4, TB, DB), BF),
+            pltpu.VMEM((2, 2, 2, 4, TB, DB), BF),
+            pltpu.VMEM((2, 2, 2, 4, TB, DB), BF),
+            pltpu.VMEM((2, 4, TB, HB), BF),
+            pltpu.VMEM((2, 4, TB, HB), BF),
             pltpu.SemaphoreType.DMA((N_SEMS,)),
             pltpu.SemaphoreType.DMA((N_SEMS,)),
         ],

time: 152 us -> 158 us (1.039)
  Pallas kernels: 148 us -> 155 us
    pallas_call x1, Pallas kernels: 148 us -> 155 us  [local(): pl.pallas_call(kernel, out_shape=jax.ShapeDtypeStruct((4 * TB, DB), BF),...]
where the time goes in v2:
time: 158 us
  Pallas kernels  155 us (98%)
  local copies, waits for them, and re-layouts  2.89 us (2%)
    pallas_call x1, Pallas kernels, local(): pl.pallas_call(kernel, out_shape=jax.ShapeDtypeStruct((4 * TB, DB), BF),...  155 us

profile of v2, /device:TPU:6, one launch (start us, length us, event | category | flops | bytes accessed | tf_op | source)
XLA Modules:
  0.0 157.8 jit_solution(16521910603336156346)
XLA Ops:
  0.0 1.2 reshape.3.gain
  1.2 154.9 %shard_map.55 = bf16[512,256]{1,0:T(8,128)(2,1)} custom-call(bf16[512,256]{1,0:T(8,128)(2,1)} %tok.1, bf16[1,256]{1,0:T(2,128)(2,1)} %reshape.3.gain, bf16[256,640]{1,0:T(8,128)(2,1)} %gw.1, bf16[256,640]{1,0:T(8,128)(2,1)} %lw.1, bf16[640,256]{1,0:T(8,128)(2,1)} %ow.1), custom_call_target="tpu_custom_call" | custom-call | tf_op jit(solution)/shard_map/pallas_call | solution.py:387
  156.2 1.7 %copy.7 = bf16[512,256]{1,0:T(8,128)(2,1)} copy(bf16[512,256]{1,0:T(8,128)(2,1)} %shard_map.55) | data formatting | bytes 524288

commit v3 on v2

v3 whole, which is shorter than its diff:
```python
import jax
import jax.numpy as jnp
from jax import lax
from jax.experimental import pallas as pl
from jax.experimental.pallas import tpu as pltpu
from jax.sharding import PartitionSpec as P

MESH = pl.DeviceIdType.MESH
BF, F32 = jnp.bfloat16, jnp.float32
FB = 160
DB = 256
HB = DB // 2
TB = 128
GR = 16
N_SEMS = 320
NT = (((1,), (1,)), ((), ()))


def wrap(v, n):
    return lax.rem(v + n, n)


def kernel(
    tok, gain, gw, lw, ow, out,
    wt, gl, w2, tst, tks, nrm, acc, hid, part, stx, srx, rtx, rrx, fin, land, send, recv,
):
    row, col = lax.axis_index("row"), lax.axis_index("col")
    zh, y = lax.div(row, 4), lax.rem(row, 4)
    zl, x, k = lax.div(col, 8), lax.rem(lax.div(col, 2), 4), lax.rem(col, 2)
    z = zh * 2 + zl

    def device(dz=0, dy=0, dx=0, dk=0):
        nz, ny, nx = wrap(z + dz, 8), wrap(y + dy, 4), wrap(x + dx, 4)
        return (lax.div(nz, 2) * 4 + ny, lax.rem(nz, 2) * 8 + nx * 2 + lax.rem(k + dk, 2))

    peers = (
        [device(dz=d) for d in (1, -1, 2, -2, 4)]
        + [device(dx=d) for d in (1, -1, 2)]
        + [device(dy=d) for d in (1, -1)]
        + [device(dk=1)]
    )
    barrier = pltpu.get_barrier_semaphore()
    for peer in peers:
        pl.semaphore_signal(barrier, inc=1, device_id=peer, device_id_type=MESH)

    wt[0] = gw[...].T
    wt[1] = lw[...].T
    for i in range(4):
        tst[i, 0:TB] = tok[i * TB : (i + 1) * TB]
        tst[i, TB : TB + GR] = jnp.broadcast_to(gain[...], (GR, DB))
    pl.semaphore_wait(barrier, len(peers))

    ids, sent = {}, []

    def copy_of(name, src, dst, to):
        i = ids.setdefault(name, len(ids))
        return pltpu.make_async_remote_copy(
            src_ref=src, dst_ref=dst, send_sem=send.at[i], recv_sem=recv.at[i],
            device_id=to, device_id_type=MESH,
        )

    def push(name, src, dst, to):
        copy = copy_of(name, src, dst, to)
        copy.start()
        sent.append(copy)

    def arrive(name, dst):
        copy_of(name, dst, dst, device(dk=1)).wait_recv()

    def token_block(dz):
        nz = wrap(z + dz, 8)
        return tks.at[lax.rem(nz, 2), k, lax.div(nz, 2)]

    def token_block_other(dz):
        nz = wrap(z + dz, 8)
        return tks.at[lax.rem(nz, 2), 1 - k, lax.div(nz, 2)]

    for e in (1, 3, 2):
        push(("ta", 4 - e), tst.at[wrap(x + e, 4)], tks.at[zl, k, zh, x], device(dx=e))

    def rows_for(d):
        return pl.ds(pl.multiple_of(wrap(zh + d, 4) * FB, 16), FB)

    def exchange_inputs(e):
        push(("gz", 4 - e), wt.at[:, rows_for(e), :], gl.at[zh, y, :, x], device(dz=2 * e))

    def exchange_outputs():
        for c in range(2):
            for e in (1, 3, 2):
                half = pl.ds(c * HB, HB)
                push(("wz", c, 4 - e), ow.at[rows_for(e), half], w2.at[c, zh, y, x], device(dz=2 * e))

    exchange_inputs(1)
    exchange_inputs(3)
    gl[zh, y, :, x] = wt[:, rows_for(0), :]
    for c in range(2):
        w2[c, zh, y, x] = ow[rows_for(0), c * HB : (c + 1) * HB]
    tks[zl, k, zh, x] = tst[x]

    class Unit:
        def __init__(self, kind, u, tag, first, way):
            self.kind, self.u, self.first, self.way = kind, u, first, way
            self.tag = (kind, tag)
            self.p, self.q = (x, y) if first == "x" else (y, x)

        def block(self, df, ds):
            f, s = wrap(self.p + df, 4), wrap(self.q + ds, 4)
            yy, xx = (s, f) if self.first == "x" else (f, s)
            if self.kind < 2:
                return gl.at[self.u, yy, self.kind, xx]
            return w2.at[self.kind - 2, self.u, yy, xx]

        def along(self, step, second=False):
            return device(dx=step) if (self.first == "x") != second else device(dy=step)

        def go(self, name, j, df, ds, step, second=False):
            ref = self.block(df, ds)
            push((self.tag, name, j), ref, ref, self.along(step, second))

        def get(self, name, j, df, ds):
            arrive((self.tag, name, j), self.block(df, ds))

        def spread(self, j):
            df = (0, -1, 1, 2)[j]
            self.go("L", j, df, 0, 1, True)
            self.go("R", j, df, 0, -1, True)

        def a0(self):
            self.go("l", 0, 0, 0, 1)
            self.go("r", 0, 0, 0, -1)
            self.spread(0)

        def a1l(self):
            self.get("l", 0, -1, 0)
            if self.way > 0:
                self.go("o", 0, -1, 0, 1)
            self.spread(1)

        def a1r(self):
            self.get("r", 0, 1, 0)
            if self.way < 0:
                self.go("o", 0, 1, 0, -1)
            self.spread(2)

        def a2(self):
            self.get("o", 0, 2, 0)
            self.spread(3)

        def b(self, j):
            df = (0, -1, 1, 2)[j]
            if j in (0, 3):
                self.get("L", j, df, -1)
                self.go("O", j, df, -1, 1, True)
            else:
                self.get("R", j, df, 1)
                self.go("O", j, df, 1, -1, True)

        def end(self):
            for j, df in enumerate((0, -1, 1, 2)):
                if j in (0, 3):
                    self.get("R", j, df, 1)
                else:
                    self.get("L", j, df, -1)
                self.get("O", j, df, 2)

    def unit_of(d):
        return wrap(zh + d, 4)

    def pair(n, d):
        way = 1 if n % 2 == 0 else -1
        return [Unit(0, unit_of(d), d, "x", way), Unit(1, unit_of(d), d, "y", way)]

    g = [pair(n, d) for n, d in enumerate((0, 1, 3, 2))]
    v = [
        [
            [Unit(2 + c, h, h, "x", 1 - 2 * h), Unit(2 + c, 2 + h, 2 + h, "y", 1 - 2 * h)]
            for h in range(2)
        ]
        for c in range(2)
    ]

    def weights_in(d):
        arrive(("gz", d), gl.at[unit_of(d), y, :, x])

    def outputs_in(c):
        for d in (1, 3, 2):
            arrive(("wz", c, d), w2.at[c, unit_of(d), y, x])

    def tokens_first():
        for d in (1, 3, 2):
            arrive(("ta", d), tks.at[zl, k, zh, wrap(x + d, 4)])
        own = token_block(0)
        push(("tm", 1), own, own, device(dz=-1))
        push(("tp", 1), own, own, device(dz=1))
        push(("s", 0), own, own, device(dk=1))
        exchange_inputs(2)

    def tokens_down(m):
        block = token_block(m)
        arrive(("tm", m), block)
        if m < 4:
            push(("tm", m + 1), block, block, device(dz=-1))
        push(("s", m), block, block, device(dk=1))

    def tokens_up(m):
        block = token_block(-m)
        arrive(("tp", m), block)
        if m < 3:
            push(("tp", m + 1), block, block, device(dz=1))
        push(("s", -m), block, block, device(dk=1))
        if m == 2:
            exchange_outputs()

    def tokens_last():
        for m in (0, 1, -1, 2, -2, 3, -3, 4):
            arrive(("s", m), token_block_other(m))

    def normalise(h):
        spots = [(a, b, c) for a in range(2) for b in range(2) for c in range(4)]

        total = jnp.zeros((TB, DB), F32)
        for a, b, c in spots:
            v = tks[a, b, h, c, 0:TB, :].astype(F32)
            total = total + v * v
        mean = jnp.sum(total, axis=1, keepdims=True) * (1.0 / 4096.0)
        scale = lax.rsqrt(mean + 1e-06)
        for a, b, c in spots:
            v = tks[a, b, h, c, 0:TB, :].astype(F32)
            g = tks[a, b, h, c, TB : TB + GR, :].astype(F32)[0:1, :]
            nrm[a * 8 + c * 2 + b, h * TB : (h + 1) * TB, :] = (v * scale * g).astype(BF)

    def project(n, t):
        u = g[n][0].u
        for a in range(2):
            right = gl[u, t, a].reshape(4 * FB, DB)
            acc[a] += lax.dot_general(nrm[u * 4 + t], right, NT, preferred_element_type=F32)

    def activate(q):
        @pl.loop(2 * q, 2 * q + 2)
        def _(t):
            rows = pl.ds(pl.multiple_of(t * 64, 64), 64)
            hid[rows, :] = (jax.nn.gelu(acc[0, rows, :], approximate=True) * acc[1, rows, :]).astype(BF)

    def terms(c, h, mine):
        core = k if mine else 1 - k

        @pl.loop(0, 2)
        def _(a):
            blocks = [w2[c, 2 * a + h, 2 * i + core].reshape(4 * FB, HB) for i in range(2)]
            right = jnp.concatenate(blocks, axis=1)
            term = jnp.dot(hid[...], right, preferred_element_type=F32)
            if mine:
                part[c, h, a] = term
            else:
                stx[c, h, a] = term.astype(BF)

        if not mine:
            push(("c", c, h), stx.at[c, h], srx.at[c, h], device(dk=1))

    def ring_value(c, h, dz):
        nz = wrap(z + dz, 8)
        a, rows = lax.rem(nz, 2), pl.ds(pl.multiple_of(lax.div(nz, 2) * TB, TB), TB)
        return part[c, h, a, rows, :] + srx[c, h, a, rows, :].astype(F32)

    def ring_step(c, h, s):
        if s == 0:
            arrive(("c", c, h), srx.at[c, h])
        for way in (0, 1):
            length = 4 if h == way else 3
            if s >= length:
                continue
            sign = 1 if way == 0 else -1
            value = ring_value(c, h, sign * (length - s))
            if s > 0:
                arrive(("r", c, h, way, s - 1), rrx.at[c, h, way, s - 1])
                value = value + rrx[c, h, way, s - 1].astype(F32)
            rtx[c, h, way, s] = value.astype(BF)
            push(("r", c, h, way, s), rtx.at[c, h, way, s], rrx.at[c, h, way, s], device(dz=sign))

    def ring_end(c, h):
        value = ring_value(c, h, 0)
        for way in (0, 1):
            last = 3 if h == way else 2
            arrive(("r", c, h, way, last), rrx.at[c, h, way, last])
            value = value + rrx[c, h, way, last].astype(F32)
        for i in range(2):
            fin[c, 2 * h + i] = value[:, i * HB : (i + 1) * HB].astype(BF)

    def hand_over(c):
        for e in (1, 3, 2):
            push(("f", c, 4 - e), fin.at[c, wrap(x + e, 4)], land.at[c, x], device(dx=e))
        land[c, x] = fin[c, x]

    def finish(c):
        for d in (1, 3, 2):
            arrive(("f", c, d), land.at[c, wrap(x + d, 4)])
        out[:, c * HB : (c + 1) * HB] = land[c].reshape(4 * TB, HB)

    acc[...] = jnp.zeros_like(acc)
    g[0][0].a0()
    g[0][1].a0()
    g[0][0].b(0)
    g[0][0].a1r()
    g[0][1].a1l()
    g[0][1].a1r()
    tokens_first()
    g[0][0].a1l()
    g[0][0].b(2)
    g[0][1].b(1)
    weights_in(3)
    weights_in(1)
    g[1][0].a0()
    g[1][1].a0()
    g[0][1].b(0)
    g[0][1].a2()
    g[0][1].b(2)
    g[0][0].b(1)
    g[1][0].b(0)
    g[1][0].a1r()
    g[0][0].a2()
    tokens_down(1)
    tokens_up(1)
    g[1][1].a1l()
    g[1][0].a1l()
    g[1][1].a1r()
    g[2][0].a0()
    g[1][1].b(0)
    g[2][1].a0()
    g[1][0].b(2)
    g[0][0].b(3)
    g[1][0].a2()
    g[0][1].b(3)
    g[1][1].b(1)
    tokens_down(2)
    g[1][0].b(1)
    g[2][0].b(0)
    g[1][1].b(2)
    g[1][1].a2()
    g[2][1].a1l()
    g[2][0].a1r()
    g[2][0].a1l()
    g[0][0].end()
    g[2][1].a1r()
    g[1][0].b(3)
    g[2][1].b(0)
    weights_in(2)
    tokens_down(3)
    g[3][0].a0()
    g[0][1].end()
    g[2][1].a2()
    g[1][1].b(3)
    g[3][1].a0()
    g[2][1].b(1)
    tokens_up(2)
    g[2][0].b(2)
    g[2][1].b(2)
    g[2][0].a2()
    g[2][0].b(1)
    g[1][0].end()
    g[3][0].a1r()
    tokens_down(4)
    g[3][0].b(0)
    g[3][1].a1r()
    g[3][1].a1l()
    g[3][0].a1l()
    tokens_up(3)
    g[2][0].b(3)
    g[2][1].b(3)
    tokens_last()
    normalise(0)
    normalise(1)
    g[3][0].a2()
    normalise(2)
    g[3][0].b(2)
    g[3][1].b(0)
    normalise(3)
    g[3][1].b(2)
    project(0, 0)
    g[3][1].a2()
    project(0, 1)
    outputs_in(0)
    g[3][1].b(1)
    v[0][0][0].a0()
    v[0][0][1].a0()
    project(0, 2)
    g[3][0].b(1)
    project(0, 3)
    g[1][1].end()
    g[3][0].b(3)
    project(1, 0)
    project(1, 1)
    project(1, 2)
    v[0][0][0].b(0)
    project(1, 3)
    v[0][0][1].a1l()
    g[2][0].end()
    g[2][1].end()
    project(2, 0)
    outputs_in(1)
    project(2, 1)
    g[3][1].b(3)
    v[0][0][1].a1r()
    project(2, 2)
    v[0][0][0].a1l()
    v[0][0][0].a1r()
    v[0][1][0].a0()
    v[0][1][1].a0()
    project(2, 3)
    v[0][0][1].a2()
    v[0][0][1].b(0)
    g[3][0].end()
    v[0][0][1].b(1)
    v[0][0][1].b(2)
    v[0][0][0].b(1)
    g[3][1].end()
    v[0][0][0].b(2)
    v[0][1][0].a1r()
    project(3, 0)
    project(3, 1)
    v[0][1][0].b(0)
    project(3, 2)
    v[0][0][0].a2()
    v[0][1][1].a1l()
    v[0][1][1].a1r()
    v[1][0][0].a0()
    v[0][1][0].a1l()
    v[1][0][1].a0()
    project(3, 3)
    activate(0)
    v[0][1][1].b(0)
    activate(1)
    v[0][0][1].b(3)
    v[0][1][0].a2()
    activate(2)
    v[0][1][0].b(2)
    activate(3)
    v[0][0][0].b(3)
    v[0][1][1].b(1)
    v[1][0][0].b(0)
    v[0][1][1].b(2)
    v[0][1][1].a2()
    v[1][0][0].a1r()
    v[1][0][1].a1l()
    v[1][0][0].a1l()
    v[0][1][0].b(1)
    v[0][1][0].b(3)
    v[1][0][1].b(0)
    v[1][0][1].a1r()
    v[1][1][0].a0()
    v[1][1][1].a0()
    v[0][0][0].end()
    v[0][0][1].end()
    terms(0, 0, False)
    v[0][1][1].b(3)
    terms(0, 0, True)
    v[1][0][0].b(2)
    v[1][0][1].b(1)
    v[1][0][1].a2()
    v[1][0][1].b(2)
    v[1][0][0].b(1)
    v[1][0][0].a2()
    v[1][1][0].a1r()
    ring_step(0, 0, 0)
    v[0][1][0].end()
    v[1][1][0].b(0)
    v[1][1][1].a1r()
    v[1][1][1].a1l()
    v[1][1][0].a1l()
    v[1][0][0].b(3)
    v[1][1][1].b(0)
    ring_step(0, 0, 1)
    v[1][1][0].a2()
    v[0][1][1].end()
    terms(0, 1, False)
    v[1][0][1].b(3)
    v[1][1][0].b(2)
    v[1][1][1].b(2)
    terms(0, 1, True)
    v[1][1][1].b(1)
    v[1][1][1].a2()
    v[1][0][0].end()
    v[1][1][0].b(1)
    ring_step(0, 0, 2)
    v[1][1][0].b(3)
    ring_step(0, 1, 0)
    v[1][0][1].end()
    terms(1, 0, False)
    v[1][1][1].b(3)
    terms(1, 0, True)
    v[1][1][0].end()
    ring_step(0, 0, 3)
    ring_step(1, 0, 0)
    v[1][1][1].end()
    terms(1, 1, False)
    ring_step(0, 1, 1)
    terms(1, 1, True)
    ring_end(0, 0)
    ring_step(1, 1, 0)
    ring_step(1, 0, 1)
    ring_step(0, 1, 2)
    ring_step(1, 1, 1)
    ring_step(1, 0, 2)
    ring_step(0, 1, 3)
    ring_step(1, 1, 2)
    ring_step(1, 0, 3)
    ring_end(0, 1)
    hand_over(0)
    ring_step(1, 1, 3)
    ring_end(1, 0)
    ring_end(1, 1)
    hand_over(1)
    finish(0)
    finish(1)
    for copy in sent:
        copy.wait_send()
    assert len(ids) <= N_SEMS, len(ids)


def local(tokens, norm_gain, gate_weight, linear_weight, output_weight):
    vmem = pl.BlockSpec(memory_space=pltpu.VMEM)
    return pl.pallas_call(
        kernel,
        out_shape=jax.ShapeDtypeStruct((4 * TB, DB), BF),
        in_specs=[vmem] * 5,
        out_specs=vmem,
        scratch_shapes=[
            pltpu.VMEM((2, 4 * FB, DB), BF),
            pltpu.VMEM((4, 4, 2, 4, FB, DB), BF),
            pltpu.VMEM((2, 4, 4, 4, FB, HB), BF),
            pltpu.VMEM((4, TB + GR, DB), BF),
            pltpu.VMEM((2, 2, 4, 4, TB + GR, DB), BF),
            pltpu.VMEM((16, 4 * TB, DB), BF),
            pltpu.VMEM((2, 4 * TB, 4 * FB), F32),
            pltpu.VMEM((4 * TB, 4 * FB), BF),
            pltpu.VMEM((2, 2, 2, 4 * TB, DB), F32),
            pltpu.VMEM((2, 2, 2, 4 * TB, DB), BF),
            pltpu.VMEM((2, 2, 2, 4 * TB, DB), BF),
            pltpu.VMEM((2, 2, 2, 4, TB, DB), BF),
            pltpu.VMEM((2, 2, 2, 4, TB, DB), BF),
            pltpu.VMEM((2, 4, TB, HB), BF),
            pltpu.VMEM((2, 4, TB, HB), BF),
            pltpu.SemaphoreType.DMA((N_SEMS,)),
            pltpu.SemaphoreType.DMA((N_SEMS,)),
        ],
        compiler_params=pltpu.CompilerParams(
            collective_id=0, has_side_effects=True, vmem_limit_bytes=60 * 1024 * 1024
        ),
    )(tokens, norm_gain.reshape(1, DB), gate_weight, linear_weight, output_weight)


def solution(mesh):
    return jax.shard_map(
        local,
        mesh=mesh,
        in_specs=(P("row", "col"), P("col"), P("row", "col"), P("row", "col"), P("col", "row")),
        out_specs=P("row", "col"),
        check_vma=False,
    )
```

time: 158 us -> 134 us (0.85)
  Pallas kernels: 155 us -> 131 us
    pallas_call x1, Pallas kernels: 155 us -> 131 us  [local(): pl.pallas_call(kernel, out_shape=jax.ShapeDtypeStruct((4 * TB, DB), BF),...]
where the time goes in v3:
time: 134 us
  Pallas kernels  131 us (98%)
  local copies, waits for them, and re-layouts  2.89 us (2%)
    pallas_call x1, Pallas kernels, local(): pl.pallas_call(kernel, out_shape=jax.ShapeDtypeStruct((4 * TB, DB), BF),...  131 us

profile of v3, /device:TPU:6, one launch (start us, length us, event | category | flops | bytes accessed | tf_op | source)
XLA Modules:
  0.0 133.5 jit_solution(13968533698624960281)
XLA Ops:
  0.0 1.2 reshape.3.gain
  1.2 130.6 %shard_map.55 = bf16[512,256]{1,0:T(8,128)(2,1)} custom-call(bf16[512,256]{1,0:T(8,128)(2,1)} %tok.1, bf16[1,256]{1,0:T(2,128)(2,1)} %reshape.3.gain, bf16[256,640]{1,0:T(8,128)(2,1)} %gw.1, bf16[256,640]{1,0:T(8,128)(2,1)} %lw.1, bf16[640,256]{1,0:T(8,128)(2,1)} %ow.1), custom_call_target="tpu_custom_call" | custom-call | tf_op jit(solution)/shard_map/pallas_call | solution.py:521
  131.8 1.7 %copy.7 = bf16[512,256]{1,0:T(8,128)(2,1)} copy(bf16[512,256]{1,0:T(8,128)(2,1)} %shard_map.55) | data formatting | bytes 524288

commit v4 on v3

v4 whole, which is shorter than its diff:
```python
import jax
import jax.numpy as jnp
from jax import lax
from jax.experimental import pallas as pl
from jax.experimental.pallas import tpu as pltpu
from jax.sharding import PartitionSpec as P

MESH = pl.DeviceIdType.MESH
BF, F32 = jnp.bfloat16, jnp.float32
FB = 160
DB = 256
HB = DB // 2
TB = 128
GR = 16
N_SEND, N_RECV = 15, 190
NT = (((1,), (1,)), ((), ()))

G_WAYS = ((("x", -1), ("y", 1)), (("x", 1), ("y", -1)), (("x", -1), ("y", 1)), (("x", 1), ("y", -1)))
V_WAYS = (((("x", 1), ("y", 1)), (("x", -1), ("y", -1))), ((("x", -1), ("y", 1)), (("x", 1), ("x", -1))))


def wrap(v, n):
    return lax.rem(v + n, n)


def kernel(
    tok, gain, gw, lw, ow, out,
    wt, gl, w2, tst, tks, nrm, acc, hid, part, stx, srx, rtx, rrx, own_tx, land, send, recv,
):
    row, col = lax.axis_index("row"), lax.axis_index("col")
    zh, y = lax.div(row, 4), lax.rem(row, 4)
    zl, x, k = lax.div(col, 8), lax.rem(lax.div(col, 2), 4), lax.rem(col, 2)
    z = zh * 2 + zl

    def device(dz=0, dy=0, dx=0, dk=0):
        nz, ny, nx = wrap(z + dz, 8), wrap(y + dy, 4), wrap(x + dx, 4)
        return (lax.div(nz, 2) * 4 + ny, lax.rem(nz, 2) * 8 + nx * 2 + lax.rem(k + dk, 2))

    def owner(dz, nx):
        nz = wrap(z + dz, 8)
        return (lax.div(nz, 2) * 4 + y, lax.rem(nz, 2) * 8 + nx * 2 + k)

    peers = (
        [device(dz=d) for d in (1, -1, 2, -2, 4)]
        + [device(dx=d) for d in (1, -1, 2)]
        + [device(dz=d, dx=e) for d in (1, -1) for e in (1, -1, 2)]
        + [device(dy=d) for d in (1, -1)]
        + [device(dk=1)]
    )
    barrier = pltpu.get_barrier_semaphore()
    for peer in peers:
        pl.semaphore_signal(barrier, inc=1, device_id=peer, device_id_type=MESH)

    wt[0] = gw[...].T
    wt[1] = lw[...].T
    pl.semaphore_wait(barrier, len(peers))

    ids, kinds = {}, {}

    def copy_of(name, kind, src, dst, to):
        i = ids.setdefault(name, len(ids))
        o = kinds.setdefault(kind, len(kinds))
        return pltpu.make_async_remote_copy(
            src_ref=src, dst_ref=dst, send_sem=send.at[o], recv_sem=recv.at[i],
            device_id=to, device_id_type=MESH,
        )

    def push(name, kind, src, dst, to):
        copy_of(name, kind, src, dst, to).start()

    def arrive(name, dst):
        copy_of(name, "gz", dst, dst, device(dk=1)).wait_recv()

    def sent(kind, src):
        copy_of(("ta",), kind, src, src, device(dk=1)).wait_send()

    def token_block(dz):
        nz = wrap(z + dz, 8)
        return tks.at[lax.rem(nz, 2), k, lax.div(nz, 2)]

    def rows_for(d):
        return pl.ds(pl.multiple_of(wrap(zh + d, 4) * FB, 16), FB)

    def exchange_inputs(e):
        push(("gz", 4 - e), "gz", wt.at[:, rows_for(e), :], gl.at[zh, y, :, x], device(dz=2 * e))

    def exchange_outputs():
        for c in range(2):
            for e in (1, 3, 2):
                half = pl.ds(c * HB, HB)
                push(("wz", c), "wz", ow.at[rows_for(e), half], w2.at[c, zh, y, x], device(dz=2 * e))

    class Unit:
        def __init__(self, kind, u, tag, first, way):
            self.kind, self.u, self.first, self.way = kind, u, first, way
            self.tag = (kind, tag)
            self.p, self.q = (x, y) if first == "x" else (y, x)

        def block(self, df, ds):
            f, s = wrap(self.p + df, 4), wrap(self.q + ds, 4)
            yy, xx = (s, f) if self.first == "x" else (f, s)
            if self.kind < 2:
                return gl.at[self.u, yy, self.kind, xx]
            return w2.at[self.kind - 2, self.u, yy, xx]

        def along(self, step, second=False):
            return device(dx=step) if (self.first == "x") != second else device(dy=step)

        def go(self, name, j, df, ds, step, second=False):
            ref = self.block(df, ds)
            last = name == "O" or (name, j) in (("R", 0), ("L", 1), ("L", 2), ("R", 3))
            size = "g" if self.kind < 2 else "w"
            key = (self.tag, "end") if last else (self.tag, name, j)
            push(key, (size, second), ref, ref, self.along(step, second))

        def get(self, name, j, df, ds):
            arrive((self.tag, name, j), self.block(df, ds))

        def spread(self, j):
            df = (0, -1, 1, 2)[j]
            self.go("L", j, df, 0, 1, True)
            self.go("R", j, df, 0, -1, True)

        def a0(self):
            self.go("l", 0, 0, 0, 1)
            self.go("r", 0, 0, 0, -1)
            self.spread(0)

        def a1l(self):
            self.get("l", 0, -1, 0)
            if self.way > 0:
                self.go("o", 0, -1, 0, 1)
            self.spread(1)

        def a1r(self):
            self.get("r", 0, 1, 0)
            if self.way < 0:
                self.go("o", 0, 1, 0, -1)
            self.spread(2)

        def a2(self):
            self.get("o", 0, 2, 0)
            self.spread(3)

        def b(self, j):
            df = (0, -1, 1, 2)[j]
            if j in (0, 3):
                self.get("L", j, df, -1)
                self.go("O", j, df, -1, 1, True)
            else:
                self.get("R", j, df, 1)
                self.go("O", j, df, 1, -1, True)

        def end(self):
            eight = gl.at[0, 0:2, 0] if self.kind < 2 else w2.at[0, 0, 0:2]
            arrive((self.tag, "end"), eight)

    def unit_of(d):
        return wrap(zh + d, 4)

    def pair(n, d):
        return [Unit(i, unit_of(d), d, *G_WAYS[n][i]) for i in range(2)]

    g = [pair(n, d) for n, d in enumerate((0, 1, 3, 2))]
    v = [
        [
            [Unit(2 + c, u, u, *V_WAYS[c][h][i]) for i, u in enumerate((h, 2 + h))]
            for h in range(2)
        ]
        for c in range(2)
    ]

    def begin():
        gl[zh, y, :, x] = wt[:, rows_for(0), :]
        g[0][0].a0()
        g[0][1].a0()
        exchange_inputs(1)
        exchange_inputs(3)
        for i in range(4):
            tst[i, 0:TB] = tok[i * TB : (i + 1) * TB]
            tst[i, TB : TB + GR] = jnp.broadcast_to(gain[...], (GR, DB))
        for e in (1, 3, 2):
            push(("ta",), "ta", tst.at[wrap(x + e, 4)], tks.at[zl, k, zh, x], device(dx=e))
        tks[zl, k, zh, x] = tst[x]
        for c in range(2):
            w2[c, zh, y, x] = ow[rows_for(0), c * HB : (c + 1) * HB]
        acc[...] = jnp.zeros_like(acc)

    def weights_in(d):
        arrive(("gz", d), gl.at[unit_of(d), y, :, x])

    def outputs_in(c):
        arrive(("wz", c), w2.at[c, 0, 0, 0:3])

    def tokens_first():
        arrive(("ta",), tks.at[0, 0, 0, 0:3])
        own = token_block(0)
        push(("tm", 1), "tm", own, own, device(dz=-1))
        push(("tp", 1), "tp", own, own, device(dz=1))
        push(("s",), "s", own, own, device(dk=1))
        exchange_inputs(2)

    def tokens_down(m):
        block = token_block(m)
        arrive(("tm", m), block)
        if m < 4:
            push(("tm", m + 1), "tm", block, block, device(dz=-1))
        push(("s",), "s", block, block, device(dk=1))

    def tokens_up(m):
        block = token_block(-m)
        arrive(("tp", m), block)
        if m < 3:
            push(("tp", m + 1), "tp", block, block, device(dz=1))
        push(("s",), "s", block, block, device(dk=1))
        if m == 2:
            exchange_outputs()

    def tokens_last():
        arrive(("s",), tks.at[:, 0])

    def normalise(h):
        spots = [(a, b, c) for a in range(2) for b in range(2) for c in range(4)]

        total = jnp.zeros((TB, DB), F32)
        for a, b, c in spots:
            v = tks[a, b, h, c, 0:TB, :].astype(F32)
            total = total + v * v
        mean = jnp.sum(total, axis=1, keepdims=True) * (1.0 / 4096.0)
        scale = lax.rsqrt(mean + 1e-06)
        for a, b, c in spots:
            v = tks[a, b, h, c, 0:TB, :].astype(F32)
            g = tks[a, b, h, c, TB : TB + GR, :].astype(F32)[0:1, :]
            nrm[a * 8 + c * 2 + b, h * TB : (h + 1) * TB, :] = (v * scale * g).astype(BF)

    def project(n, t):
        u = g[n][0].u
        for a in range(2):
            right = gl[u, t, a].reshape(4 * FB, DB)
            acc[a] += lax.dot_general(nrm[u * 4 + t], right, NT, preferred_element_type=F32)

    def activate(q):
        @pl.loop(2 * q, 2 * q + 2)
        def _(t):
            rows = pl.ds(pl.multiple_of(t * 64, 64), 64)
            hid[rows, :] = (jax.nn.gelu(acc[0, rows, :], approximate=True) * acc[1, rows, :]).astype(BF)

    def terms(c, h, mine):
        core = k if mine else 1 - k
        for a in range(2):
            blocks = [w2[c, 2 * a + h, 2 * i + core].reshape(4 * FB, HB) for i in range(2)]
            right = jnp.concatenate(blocks, axis=1)
            term = jnp.dot(hid[...], right, preferred_element_type=F32)
            if mine:
                part[c, h, a] = term
            else:
                stx[c, h, a] = term.astype(BF)
                push(("c", c, h), "c", stx.at[c, h, a], srx.at[c, h, a], device(dk=1))

    def ring_value(c, h, i, dz):
        nz = wrap(z + dz, 8)
        a, rows = lax.rem(nz, 2), pl.ds(pl.multiple_of(lax.div(nz, 2) * TB, TB), TB)
        lanes = pl.ds(i * HB, HB)
        return part[c, h, a, rows, lanes] + srx[c, h, a, rows, lanes].astype(F32)

    def own_share(c, h):
        for i in range(2):
            nx = 2 * h + i
            own_tx[c, nx] = ring_value(c, h, i, 0).astype(BF)

            @pl.when(x != nx)
            def _():
                push(("fo", c), "fo", own_tx.at[c, nx], land.at[c, 2, x], owner(0, nx))

            @pl.when(x == nx)
            def _():
                land[c, 2, nx] = own_tx[c, nx]

    def ring_step(c, h, i, s):
        if s == 0 and i == 0:
            arrive(("c", c, h), srx.at[c, h])
        for way in (0, 1):
            length = 4 if h == way else 3
            if s >= length:
                continue
            sign = 1 if way == 0 else -1
            value = ring_value(c, h, i, sign * (length - s))
            if s > 0:
                arrive(("r", c, h, i, way, s - 1), rrx.at[c, h, i, way, s - 1])
                value = value + rrx[c, h, i, way, s - 1].astype(F32)
            rtx[c, h, i, way, s] = value.astype(BF)
            src = rtx.at[c, h, i, way, s]
            if s < length - 1:
                push(("r", c, h, i, way, s), ("r", length), src, rrx.at[c, h, i, way, s], device(dz=sign))
            else:
                push(("fr", c), "fr", src, land.at[c, way, x], owner(sign, 2 * h + i))

    def finish(c):
        arrive(("fr", c), land.at[c, 0:2])
        arrive(("fo", c), land.at[c, 2, 0:3])
        for nx in range(4):
            total = land[c, 0, nx].astype(F32) + land[c, 1, nx].astype(F32)
            total = total + land[c, 2, nx].astype(F32)
            out[nx * TB : (nx + 1) * TB, c * HB : (c + 1) * HB] = total.astype(BF)

    begin()
    g[0][0].a1l()
    g[0][0].a1r()
    g[0][0].b(0)
    g[0][1].b(0)
    g[0][1].a1l()
    g[0][1].a1r()
    g[0][0].b(1)
    g[0][0].a2()
    g[0][0].b(2)
    weights_in(3)
    weights_in(1)
    g[1][0].a0()
    g[0][1].b(1)
    tokens_first()
    g[0][1].b(2)
    g[0][1].a2()
    g[1][1].a0()
    g[1][0].a1r()
    g[0][0].b(3)
    g[1][0].b(0)
    g[1][0].a1l()
    g[1][1].a1l()
    g[1][1].a1r()
    g[0][1].b(3)
    g[1][0].b(2)
    g[1][1].b(0)
    tokens_down(1)
    tokens_up(1)
    g[0][0].end()
    g[1][0].b(1)
    g[2][0].a0()
    g[1][0].a2()
    g[1][1].b(1)
    g[1][1].a2()
    g[1][1].b(2)
    g[2][1].a0()
    g[2][0].a1r()
    g[2][0].b(0)
    g[0][1].end()
    g[1][0].b(3)
    g[2][1].a1l()
    tokens_down(2)
    g[2][0].a1l()
    g[2][1].a1r()
    g[1][1].b(3)
    g[2][0].b(2)
    g[2][1].b(0)
    g[2][0].a2()
    weights_in(2)
    g[1][0].end()
    g[2][0].b(1)
    g[3][0].a0()
    g[2][1].b(1)
    g[2][1].a2()
    g[2][1].b(2)
    g[3][1].a0()
    g[1][1].end()
    g[3][0].a1r()
    g[2][0].b(3)
    tokens_down(3)
    tokens_up(2)
    g[3][0].b(0)
    g[3][0].a1l()
    g[3][1].a1l()
    g[3][1].a1r()
    g[2][1].b(3)
    g[3][0].b(2)
    g[3][1].b(0)
    g[2][0].end()
    g[3][0].b(1)
    g[3][0].a2()
    g[3][1].b(1)
    g[3][1].a2()
    g[3][1].b(2)
    tokens_down(4)
    tokens_up(3)
    g[3][0].b(3)
    g[2][1].end()
    tokens_last()
    normalise(0)
    normalise(1)
    normalise(2)
    outputs_in(0)
    g[3][1].b(3)
    v[0][0][0].a0()
    v[0][0][1].a0()
    normalise(3)
    v[0][1][0].a0()
    project(0, 0)
    v[0][1][1].a0()
    project(0, 1)
    project(0, 2)
    v[0][0][0].a1r()
    v[0][0][0].b(0)
    project(0, 3)
    v[0][0][1].a1l()
    v[0][0][1].a1r()
    project(1, 0)
    outputs_in(1)
    v[0][0][0].a1l()
    v[0][1][0].a1r()
    v[0][1][0].b(0)
    project(1, 1)
    v[0][0][1].b(0)
    v[0][1][1].a1l()
    v[0][1][1].a1r()
    project(1, 2)
    v[0][0][0].b(2)
    v[0][1][0].a1l()
    project(1, 3)
    v[0][0][1].b(1)
    v[0][1][1].b(0)
    project(2, 0)
    v[0][0][0].b(1)
    v[0][0][1].b(2)
    project(2, 1)
    v[0][0][1].a2()
    v[0][1][0].a2()
    v[0][1][0].b(2)
    project(2, 2)
    v[0][1][1].b(1)
    v[0][1][1].a2()
    project(2, 3)
    v[0][0][0].a2()
    g[3][0].end()
    v[0][1][1].b(2)
    g[3][1].end()
    v[1][0][0].a0()
    project(3, 0)
    v[0][1][0].b(1)
    v[1][0][1].a0()
    project(3, 1)
    project(3, 2)
    v[0][1][0].b(3)
    project(3, 3)
    v[1][1][0].a0()
    v[0][0][0].b(3)
    activate(0)
    activate(1)
    v[0][0][1].b(3)
    v[1][0][0].b(0)
    activate(2)
    v[0][1][1].b(3)
    v[1][0][1].a1l()
    v[1][1][1].a0()
    activate(3)
    v[1][0][0].a1l()
    v[1][0][0].a1r()
    v[0][1][0].end()
    v[1][0][1].b(0)
    v[1][1][0].b(0)
    v[1][0][1].a1r()
    v[1][1][0].a1l()
    v[0][0][0].end()
    v[1][1][0].a1r()
    v[0][0][1].end()
    terms(0, 0, False)
    v[1][0][1].b(1)
    v[1][0][1].a2()
    terms(0, 0, True)
    v[1][0][0].b(1)
    v[1][1][1].a1r()
    v[1][1][1].b(0)
    v[0][1][1].end()
    v[1][0][0].a2()
    v[1][0][0].b(2)
    terms(0, 1, False)
    v[1][0][1].b(2)
    v[1][1][0].b(1)
    v[1][1][1].a1l()
    terms(0, 1, True)
    ring_step(0, 0, 0, 0)
    ring_step(0, 0, 1, 0)
    v[1][1][0].b(2)
    own_share(0, 0)
    v[1][1][0].a2()
    v[1][1][1].a2()
    v[1][1][1].b(2)
    ring_step(0, 1, 0, 0)
    ring_step(0, 1, 1, 0)
    v[1][0][1].b(3)
    own_share(0, 1)
    ring_step(0, 0, 0, 1)
    ring_step(0, 0, 1, 1)
    v[1][0][0].b(3)
    v[1][1][1].b(1)
    v[1][0][1].end()
    ring_step(0, 1, 0, 1)
    v[1][1][0].b(3)
    ring_step(0, 1, 1, 1)
    v[1][1][1].b(3)
    ring_step(0, 0, 0, 2)
    v[1][0][0].end()
    terms(1, 0, False)
    ring_step(0, 0, 1, 2)
    terms(1, 0, True)
    v[1][1][0].end()
    ring_step(0, 1, 0, 2)
    v[1][1][1].end()
    terms(1, 1, False)
    ring_step(0, 1, 1, 2)
    terms(1, 1, True)
    ring_step(1, 0, 0, 0)
    ring_step(1, 0, 1, 0)
    ring_step(0, 0, 0, 3)
    own_share(1, 0)
    ring_step(0, 0, 1, 3)
    ring_step(1, 1, 0, 0)
    ring_step(1, 1, 1, 0)
    own_share(1, 1)
    ring_step(0, 1, 0, 3)
    ring_step(1, 0, 0, 1)
    ring_step(0, 1, 1, 3)
    ring_step(1, 0, 1, 1)
    ring_step(1, 1, 0, 1)
    ring_step(1, 1, 1, 1)
    ring_step(1, 0, 0, 2)
    ring_step(1, 0, 1, 2)
    ring_step(1, 1, 0, 2)
    ring_step(1, 1, 1, 2)
    ring_step(1, 0, 0, 3)
    ring_step(1, 0, 1, 3)
    ring_step(1, 1, 0, 3)
    ring_step(1, 1, 1, 3)
    finish(0)
    finish(1)
    for kind, src in (
        ("ta", tks.at[0, 0, 0, 0:3]),
        ("gz", gl.at[0, 0:3, :, 0]),
        ("wz", w2.at[:, 0, 0, 0:3]),
        (("g", True), gl.at[:, 0:3]),
        (("g", False), gl.at[:, 0:3, :, 0]),
        (("w", True), w2.at[:, :, 0:3]),
        (("w", False), w2.at[:, :, 0:3, 0]),
        ("tm", tks.at[0, 0]),
        ("tp", tks.at[0, 0, 0:3]),
        ("s", tks.at[0]),
        ("c", stx),
        (("r", 4), rtx.at[:, :, :, 0, 0:3]),
        (("r", 3), rtx.at[:, :, :, 0, 0:2]),
        ("fr", rtx.at[:, :, :, :, 0]),
        ("fo", own_tx.at[:, 0:3]),
    ):
        sent(kind, src)
    assert len(ids) == N_RECV and len(kinds) == N_SEND, (len(ids), len(kinds))


def local(tokens, norm_gain, gate_weight, linear_weight, output_weight):
    vmem = pl.BlockSpec(memory_space=pltpu.VMEM)
    return pl.pallas_call(
        kernel,
        out_shape=jax.ShapeDtypeStruct((4 * TB, DB), BF),
        in_specs=[vmem] * 5,
        out_specs=vmem,
        scratch_shapes=[
            pltpu.VMEM((2, 4 * FB, DB), BF),
            pltpu.VMEM((4, 4, 2, 4, FB, DB), BF),
            pltpu.VMEM((2, 4, 4, 4, FB, HB), BF),
            pltpu.VMEM((4, TB + GR, DB), BF),
            pltpu.VMEM((2, 2, 4, 4, TB + GR, DB), BF),
            pltpu.VMEM((16, 4 * TB, DB), BF),
            pltpu.VMEM((2, 4 * TB, 4 * FB), F32),
            pltpu.VMEM((4 * TB, 4 * FB), BF),
            pltpu.VMEM((2, 2, 2, 4 * TB, DB), F32),
            pltpu.VMEM((2, 2, 2, 4 * TB, DB), BF),
            pltpu.VMEM((2, 2, 2, 4 * TB, DB), BF),
            pltpu.VMEM((2, 2, 2, 2, 4, TB, HB), BF),
            pltpu.VMEM((2, 2, 2, 2, 3, TB, HB), BF),
            pltpu.VMEM((2, 4, TB, HB), BF),
            pltpu.VMEM((2, 3, 4, TB, HB), BF),
            pltpu.SemaphoreType.DMA((N_SEND,)),
            pltpu.SemaphoreType.DMA((N_RECV,)),
        ],
        compiler_params=pltpu.CompilerParams(
            collective_id=0, has_side_effects=True, vmem_limit_bytes=60 * 1024 * 1024
        ),
    )(tokens, norm_gain.reshape(1, DB), gate_weight, linear_weight, output_weight)


def solution(mesh):
    return jax.shard_map(
        local,
        mesh=mesh,
        in_specs=(P("row", "col"), P("col"), P("row", "col"), P("row", "col"), P("col", "row")),
        out_specs=P("row", "col"),
        check_vma=False,
    )
```

time: 134 us -> 126 us (0.940)
  Pallas kernels: 131 us -> 123 us
    pallas_call x1, Pallas kernels: 131 us -> 123 us  [local(): pl.pallas_call(kernel, out_shape=jax.ShapeDtypeStruct((4 * TB, DB), BF),...]
where the time goes in v4:
time: 126 us
  Pallas kernels  123 us (98%)
  local copies, waits for them, and re-layouts  2.89 us (2%)
    pallas_call x1, Pallas kernels, local(): pl.pallas_call(kernel, out_shape=jax.ShapeDtypeStruct((4 * TB, DB), BF),...  123 us

profile of v4, /device:TPU:6, one launch (start us, length us, event | category | flops | bytes accessed | tf_op | source)
XLA Modules:
  0.0 125.8 jit_solution(10654573944470391634)
XLA Ops:
  0.0 1.2 reshape.3.gain
  1.2 122.9 %shard_map.55 = bf16[512,256]{1,0:T(8,128)(2,1)} custom-call(bf16[512,256]{1,0:T(8,128)(2,1)} %tok.1, bf16[1,256]{1,0:T(2,128)(2,1)} %reshape.3.gain, bf16[256,640]{1,0:T(8,128)(2,1)} %gw.1, bf16[256,640]{1,0:T(8,128)(2,1)} %lw.1, bf16[640,256]{1,0:T(8,128)(2,1)} %ow.1), custom_call_target="tpu_custom_call" | custom-call | tf_op jit(solution)/shard_map/pallas_call | solution.py:556
  124.2 1.7 %copy.7 = bf16[512,256]{1,0:T(8,128)(2,1)} copy(bf16[512,256]{1,0:T(8,128)(2,1)} %shard_map.55) | data formatting | bytes 524288

commit v5 on v4

--- a/solution.py
+++ b/solution.py
@@ -16,7 +16,7 @@
 NT = (((1,), (1,)), ((), ()))
 
 G_WAYS = ((("x", -1), ("y", 1)), (("x", 1), ("y", -1)), (("x", -1), ("y", 1)), (("x", 1), ("y", -1)))
-V_WAYS = (((("x", 1), ("y", 1)), (("x", -1), ("y", -1))), ((("x", -1), ("y", 1)), (("x", 1), ("x", -1))))
+V_WAYS = (((("x", -1), ("y", 1)), (("x", -1), ("y", -1))), ((("x", -1), ("y", 1)), (("x", 1), ("x", -1))))
 
 
 def wrap(v, n):
@@ -219,19 +219,22 @@
     def tokens_last():
         arrive(("s",), tks.at[:, 0])
 
-    def normalise(h):
+    def normalise():
         spots = [(a, b, c) for a in range(2) for b in range(2) for c in range(4)]
 
-        total = jnp.zeros((TB, DB), F32)
-        for a, b, c in spots:
-            v = tks[a, b, h, c, 0:TB, :].astype(F32)
-            total = total + v * v
-        mean = jnp.sum(total, axis=1, keepdims=True) * (1.0 / 4096.0)
-        scale = lax.rsqrt(mean + 1e-06)
-        for a, b, c in spots:
-            v = tks[a, b, h, c, 0:TB, :].astype(F32)
-            g = tks[a, b, h, c, TB : TB + GR, :].astype(F32)[0:1, :]
-            nrm[a * 8 + c * 2 + b, h * TB : (h + 1) * TB, :] = (v * scale * g).astype(BF)
+        @pl.loop(0, 4)
+        def _(h):
+            total = jnp.zeros((TB, DB), F32)
+            for a, b, c in spots:
+                v = tks[a, b, h, c, 0:TB, :].astype(F32)
+                total = total + v * v
+            mean = jnp.sum(total, axis=1, keepdims=True) * (1.0 / 4096.0)
+            scale = lax.rsqrt(mean + 1e-06)
+            rows = pl.ds(pl.multiple_of(h * TB, TB), TB)
+            for a, b, c in spots:
+                v = tks[a, b, h, c, 0:TB, :].astype(F32)
+                g = tks[a, b, h, c, TB : TB + GR, :].astype(F32)[0:1, :]
+                nrm[a * 8 + c * 2 + b, rows, :] = (v * scale * g).astype(BF)
 
     def project(n, t):
         u = g[n][0].u
@@ -383,14 +386,11 @@
     g[3][0].b(3)
     g[2][1].end()
     tokens_last()
-    normalise(0)
-    normalise(1)
-    normalise(2)
     outputs_in(0)
     g[3][1].b(3)
     v[0][0][0].a0()
     v[0][0][1].a0()
-    normalise(3)
+    normalise()
     v[0][1][0].a0()
     project(0, 0)
     v[0][1][1].a0()
@@ -411,6 +411,7 @@
     v[0][1][1].a1l()
     v[0][1][1].a1r()
     project(1, 2)
+    v[0][0][0].a2()
     v[0][0][0].b(2)
     v[0][1][0].a1l()
     project(1, 3)
@@ -418,105 +419,104 @@
     v[0][1][1].b(0)
     project(2, 0)
     v[0][0][0].b(1)
+    project(2, 1)
     v[0][0][1].b(2)
-    project(2, 1)
     v[0][0][1].a2()
-    v[0][1][0].a2()
     v[0][1][0].b(2)
     project(2, 2)
-    v[0][1][1].b(1)
+    v[0][1][0].a2()
     v[0][1][1].a2()
     project(2, 3)
-    v[0][0][0].a2()
+    v[0][1][1].b(1)
     g[3][0].end()
+    g[3][1].end()
     v[0][1][1].b(2)
-    g[3][1].end()
     v[1][0][0].a0()
     project(3, 0)
+    v[1][0][1].a0()
+    v[0][0][0].b(3)
+    project(3, 1)
     v[0][1][0].b(1)
-    v[1][0][1].a0()
-    project(3, 1)
     project(3, 2)
+    project(3, 3)
+    v[0][0][1].b(3)
     v[0][1][0].b(3)
-    project(3, 3)
+    activate(0)
     v[1][1][0].a0()
-    v[0][0][0].b(3)
-    activate(0)
     activate(1)
-    v[0][0][1].b(3)
+    v[0][1][1].b(3)
     v[1][0][0].b(0)
     activate(2)
-    v[0][1][1].b(3)
+    v[1][0][0].a1l()
     v[1][0][1].a1l()
+    activate(3)
+    v[1][0][1].b(0)
+    v[0][0][0].end()
     v[1][1][1].a0()
-    activate(3)
-    v[1][0][0].a1l()
+    v[1][0][1].a1r()
+    v[0][0][1].end()
     v[1][0][0].a1r()
+    terms(0, 0, False)
+    v[1][1][0].a1l()
+    v[1][1][0].b(0)
+    terms(0, 0, True)
+    v[1][1][0].a1r()
     v[0][1][0].end()
-    v[1][0][1].b(0)
-    v[1][1][0].b(0)
-    v[1][0][1].a1r()
-    v[1][1][0].a1l()
-    v[0][0][0].end()
-    v[1][1][0].a1r()
-    v[0][0][1].end()
-    terms(0, 0, False)
+    v[1][0][0].b(1)
+    v[0][1][1].end()
+    terms(0, 1, False)
     v[1][0][1].b(1)
+    terms(0, 1, True)
     v[1][0][1].a2()
-    terms(0, 0, True)
-    v[1][0][0].b(1)
-    v[1][1][1].a1r()
-    v[1][1][1].b(0)
-    v[0][1][1].end()
-    v[1][0][0].a2()
     v[1][0][0].b(2)
-    terms(0, 1, False)
-    v[1][0][1].b(2)
-    v[1][1][0].b(1)
-    v[1][1][1].a1l()
-    terms(0, 1, True)
     ring_step(0, 0, 0, 0)
     ring_step(0, 0, 1, 0)
+    v[1][0][1].b(2)
+    v[1][1][1].a1r()
+    v[1][1][1].a1l()
+    v[1][1][0].b(1)
+    v[1][1][1].b(0)
+    own_share(0, 0)
+    v[1][0][0].a2()
     v[1][1][0].b(2)
-    own_share(0, 0)
     v[1][1][0].a2()
-    v[1][1][1].a2()
-    v[1][1][1].b(2)
     ring_step(0, 1, 0, 0)
     ring_step(0, 1, 1, 0)
+    own_share(0, 1)
     v[1][0][1].b(3)
-    own_share(0, 1)
     ring_step(0, 0, 0, 1)
+    v[1][1][1].b(2)
+    v[1][1][1].a2()
     ring_step(0, 0, 1, 1)
+    v[1][1][1].b(1)
+    ring_step(0, 1, 0, 1)
+    v[1][0][1].end()
+    ring_step(0, 1, 1, 1)
     v[1][0][0].b(3)
-    v[1][1][1].b(1)
-    v[1][0][1].end()
-    ring_step(0, 1, 0, 1)
     v[1][1][0].b(3)
-    ring_step(0, 1, 1, 1)
+    ring_step(0, 0, 0, 2)
+    ring_step(0, 0, 1, 2)
     v[1][1][1].b(3)
-    ring_step(0, 0, 0, 2)
     v[1][0][0].end()
+    ring_step(0, 1, 0, 2)
     terms(1, 0, False)
-    ring_step(0, 0, 1, 2)
+    ring_step(0, 1, 1, 2)
     terms(1, 0, True)
     v[1][1][0].end()
-    ring_step(0, 1, 0, 2)
+    ring_step(0, 0, 0, 3)
     v[1][1][1].end()
     terms(1, 1, False)
-    ring_step(0, 1, 1, 2)
+    ring_step(0, 0, 1, 3)
     terms(1, 1, True)
     ring_step(1, 0, 0, 0)
     ring_step(1, 0, 1, 0)
-    ring_step(0, 0, 0, 3)
+    ring_step(0, 1, 0, 3)
     own_share(1, 0)
-    ring_step(0, 0, 1, 3)
+    ring_step(0, 1, 1, 3)
     ring_step(1, 1, 0, 0)
     ring_step(1, 1, 1, 0)
     own_share(1, 1)
-    ring_step(0, 1, 0, 3)
     ring_step(1, 0, 0, 1)
-    ring_step(0, 1, 1, 3)
     ring_step(1, 0, 1, 1)
     ring_step(1, 1, 0, 1)
     ring_step(1, 1, 1, 1)

time: 126 us -> 126 us (level)
  no operation moved by 1% of the time
where the time goes in v5:
time: 126 us
  Pallas kernels  123 us (98%)
  local copies, waits for them, and re-layouts  2.89 us (2%)
    pallas_call x1, Pallas kernels, local(): pl.pallas_call(kernel, out_shape=jax.ShapeDtypeStruct((4 * TB, DB), BF),...  123 us

profile of v5, /device:TPU:6, one launch (start us, length us, event | category | flops | bytes accessed | tf_op | source)
XLA Modules:
  0.0 125.7 jit_solution(1975219315946389896)
XLA Ops:
  0.0 1.2 reshape.3.gain
  1.2 122.8 %shard_map.55 = bf16[512,256]{1,0:T(8,128)(2,1)} custom-call(bf16[512,256]{1,0:T(8,128)(2,1)} %tok.1, bf16[1,256]{1,0:T(2,128)(2,1)} %reshape.3.gain, bf16[256,640]{1,0:T(8,128)(2,1)} %gw.1, bf16[256,640]{1,0:T(8,128)(2,1)} %lw.1, bf16[640,256]{1,0:T(8,128)(2,1)} %ow.1), custom_call_target="tpu_custom_call" | custom-call | tf_op jit(solution)/shard_map/pallas_call | solution.py:556
  124.0 1.7 %copy.7 = bf16[512,256]{1,0:T(8,128)(2,1)} copy(bf16[512,256]{1,0:T(8,128)(2,1)} %shard_map.55) | data formatting | bytes 524288

commit v6 on v5

--- a/solution.py
+++ b/solution.py
@@ -53,6 +53,7 @@
 
     wt[0] = gw[...].T
     wt[1] = lw[...].T
+    acc[...] = jnp.zeros_like(acc)
     pl.semaphore_wait(barrier, len(peers))
 
     ids, kinds = {}, {}
@@ -184,7 +185,6 @@
         tks[zl, k, zh, x] = tst[x]
         for c in range(2):
             w2[c, zh, y, x] = ow[rows_for(0), c * HB : (c + 1) * HB]
-        acc[...] = jnp.zeros_like(acc)
 
     def weights_in(d):
         arrive(("gz", d), gl.at[unit_of(d), y, :, x])
@@ -316,26 +316,26 @@
     g[0][0].b(1)
     g[0][0].a2()
     g[0][0].b(2)
+    g[0][1].b(1)
+    tokens_first()
     weights_in(3)
     weights_in(1)
     g[1][0].a0()
-    g[0][1].b(1)
-    tokens_first()
     g[0][1].b(2)
     g[0][1].a2()
     g[1][1].a0()
+    g[0][0].b(3)
     g[1][0].a1r()
-    g[0][0].b(3)
     g[1][0].b(0)
     g[1][0].a1l()
     g[1][1].a1l()
     g[1][1].a1r()
     g[0][1].b(3)
+    g[0][0].end()
     g[1][0].b(2)
     g[1][1].b(0)
     tokens_down(1)
     tokens_up(1)
-    g[0][0].end()
     g[1][0].b(1)
     g[2][0].a0()
     g[1][0].a2()
@@ -355,9 +355,9 @@
     g[2][0].b(2)
     g[2][1].b(0)
     g[2][0].a2()
-    weights_in(2)
     g[1][0].end()
     g[2][0].b(1)
+    weights_in(2)
     g[3][0].a0()
     g[2][1].b(1)
     g[2][1].a2()

time: 126 us -> 126 us (level)
  no operation moved by 1% of the time
where the time goes in v6:
time: 126 us
  Pallas kernels  123 us (98%)
  local copies, waits for them, and re-layouts  2.89 us (2%)
    pallas_call x1, Pallas kernels, local(): pl.pallas_call(kernel, out_shape=jax.ShapeDtypeStruct((4 * TB, DB), BF),...  123 us

profile of v6, /device:TPU:6, one launch (start us, length us, event | category | flops | bytes accessed | tf_op | source)
XLA Modules:
  0.0 125.5 jit_solution(17760962318902927738)
XLA Ops:
  0.0 1.2 reshape.3.gain
  1.2 122.6 %shard_map.55 = bf16[512,256]{1,0:T(8,128)(2,1)} custom-call(bf16[512,256]{1,0:T(8,128)(2,1)} %tok.1, bf16[1,256]{1,0:T(2,128)(2,1)} %reshape.3.gain, bf16[256,640]{1,0:T(8,128)(2,1)} %gw.1, bf16[256,640]{1,0:T(8,128)(2,1)} %lw.1, bf16[640,256]{1,0:T(8,128)(2,1)} %ow.1), custom_call_target="tpu_custom_call" | custom-call | tf_op jit(solution)/shard_map/pallas_call | solution.py:556
  123.8 1.7 %copy.7 = bf16[512,256]{1,0:T(8,128)(2,1)} copy(bf16[512,256]{1,0:T(8,128)(2,1)} %shard_map.55) | data formatting | bytes 524288
